TPU v7x, 32 devices: a whole 2x2x4 slice. The times are simulated.
32 devices in a mesh: ty: 4 (over y, x), tx: 8 (over z, core).
Axes of the slice: x: 2, y: 2, z: 4, core: 2. Of those that a mesh axis runs over, the one named last changes fastest.
Arguments:
- object_slices: float32 [2, 2, 1024, 2048], P(None, None, 'ty', 'tx'), may hold values from -5 to 5
- probe: float32 [2, 256, 256], replicated, may hold values from -5 to 5
- position_count: int32 [4, 8], P('ty', 'tx'), may hold values from 1 to 5, as said below
- offsets: int32 [4, 8, 5, 2], P('ty', 'tx'), may hold values from 0 to 128
- intensities: float32 [4, 8, 5, 256, 256], P('ty', 'tx'), may hold values from 0 to 2
Outputs:
- object_new: float32 [2, 2, 1024, 2048], P(None, None, 'ty', 'tx')
- probe_new: float32 [2, 256, 256], replicated
Inputs may be any that keep to these rules, and one draw needn't show every extreme that they name: `position_count`: each tile has 1 to 5 positions; some tile has exactly 5.
All inputs are finite; a program needn't handle non-finite values.
Results may differ from a plain program's by a relative error of at most 0.0003.
Values sent between devices are 32-bit elements; how exact they have to be, the bound alone decides.
No kernel may reach another device: no remote copies, remote signals or barrier semaphores. Data moves between devices by JAX's collectives and lax.ppermute only.
A program may use at most 128 MiB of HBM per device.

v0:
```python
import math

import jax
import jax.numpy as jnp
import ml_dtypes
import numpy as np
from jax import lax
from jax.experimental import pallas as pl
from jax.experimental.pallas import tpu as pltpu
from jax.sharding import PartitionSpec as P

MARGIN = 64
ITERS = 2
CHUNK = 16
SKEW = 0

chirp_rate = 0.5
object_rate = 0.5
probe_rate = 2.0


def tables(size):
    index = np.arange(size)
    four = np.exp(-2j * np.pi * (np.outer(index, index) % size) / size) / math.sqrt(size)
    centred = (index + size // 2) % size - size // 2
    kernel = np.exp(-1j * chirp_rate * np.pi * centred * centred / size)
    prop = (four.conj() * kernel[None, :]) @ four
    half = size // 2
    near, far = prop[:half, :half], prop[:half, half:]
    blocks = ((0.5 * (near + far), 0.5 * (near - far)), (four[0::2, :half], four[1::2, :half]))
    out = np.zeros((2, 2, 2, 2, size, size), ml_dtypes.bfloat16)
    for family in range(2):
        for parity in range(2):
            block = blocks[family][parity]
            left = np.block([[block.real, -block.imag], [block.imag, block.real]])
            for form, value in enumerate((left, left.T)):
                high = value.astype(np.float32).astype(ml_dtypes.bfloat16)
                low = (value - high.astype(np.float64)).astype(np.float32).astype(ml_dtypes.bfloat16)
                out[family, parity, form, 0] = high
                out[family, parity, form, 1] = low
    return out


def lane_order(size):
    out = np.zeros((size, size), ml_dtypes.bfloat16)
    half = size // 2
    for lane in range(half):
        out[2 * lane, lane] = 1
        out[2 * lane + 1, half + lane] = 1
    return np.stack([out, out.T])


def dot(left, right):
    return jnp.dot(left, right, preferred_element_type=jnp.float32)


def parts(value):
    high = value.astype(jnp.bfloat16)
    low = (value - high.astype(jnp.float32)).astype(jnp.bfloat16)
    return high, low


def thirds(value):
    first = value.astype(jnp.bfloat16)
    rest = value - first.astype(jnp.float32)
    second = rest.astype(jnp.bfloat16)
    return first, second, (rest - second.astype(jnp.float32)).astype(jnp.bfloat16)


def sort_kernel(count_ref, values_ref, order_ref, out_ref):
    out_ref[...] = jnp.zeros_like(out_ref)

    def visit(slot, carry):
        first, second, third = [dot(x, order_ref[0]) for x in thirds(values_ref[slot])]
        first, second, third = [dot(order_ref[1], x) for x in thirds((first + second) + third)]
        out_ref[slot] = (first + second) + third
        return carry

    lax.fori_loop(0, count_ref[0], visit, 0)


def common(size):
    half, quarter = size // 2, size // 4

    def at(part, start):
        return pl.ds(part * half + start, CHUNK)

    def lanes(part):
        return pl.ds(part * half, half)

    def boundary(part, start):
        return (start < quarter) == (part == 0)

    return half, at, lanes, boundary


def fold(quads):
    mixed = [[quads[0][c] + quads[1][c] for c in range(2)], [quads[0][c] - quads[1][c] for c in range(2)]]
    return [[m[0] + m[1], m[0] - m[1]] for m in mixed]


def empty():
    return [[None, None], [None, None]]


def masks(size, top, lead):
    half = size // 2
    lane = lax.broadcasted_iota(jnp.int32, (CHUNK, half), 1)
    row = lax.broadcasted_iota(jnp.int32, (CHUNK, half), 0)
    cols = (lane + MARGIN >= lead, lane - MARGIN < lead)

    def row_mask(part, start):
        inside = row + start
        return inside + MARGIN >= top if part == 0 else inside - MARGIN < top

    return cols, row_mask


def stages(size, table_ref, high_ref, low_ref, rhigh_ref, rlow_ref, mid_ref, back_ref):
    half, at, lanes, _ = common(size)

    def put(start, real, imag):
        for p in range(2):
            for q in range(2):
                for comp, value in ((0, real[p][q]), (1, imag[p][q])):
                    high, low = parts(value)
                    high_ref[q, at(p, start), lanes(comp)] = high
                    low_ref[q, at(p, start), lanes(comp)] = low

    def right(family, form):
        for q in range(2):
            weight, small = table_ref[family, q, form, 0], table_ref[family, q, form, 1]
            mid_ref[q] = dot(high_ref[q], weight) + dot(low_ref[q], weight) + dot(high_ref[q], small)
        for q in range(2):
            for p in range(2):
                for start in range(0, half, CHUNK):
                    for comp in range(2):
                        high, low = parts(mid_ref[q, at(p, start), lanes(comp)])
                        rhigh_ref[p, at(comp, start), lanes(q)] = high
                        rlow_ref[p, at(comp, start), lanes(q)] = low

    def left(family, form):
        for p in range(2):
            weight, small = table_ref[family, p, 1 - form, 0], table_ref[family, p, 1 - form, 1]
            back_ref[p] = dot(weight, rhigh_ref[p]) + dot(small, rhigh_ref[p]) + dot(weight, rlow_ref[p])

    def take(start, comp):
        return [[back_ref[p, at(comp, start), lanes(q)] for q in range(2)] for p in range(2)]

    return put, right, left, take


def window_of(size, core_ref, row_ref, col_ref, corner_ref, cols, row_mask):
    half, at, lanes, boundary = common(size)

    def window(start, k):
        out = empty()
        for r in range(2):
            other = col_ref[k, at(r, start), :]
            if boundary(r, start):
                mask = row_mask(r, start)
                other = jnp.where(mask, other, corner_ref[k, pl.ds(start, CHUNK), :])
            for c in range(2):
                own = core_ref[k, at(r, start), lanes(c)]
                if boundary(r, start):
                    own = jnp.where(mask, own, row_ref[k, pl.ds(start, CHUNK), lanes(c)])
                out[r][c] = jnp.where(cols[c], own, other)
        return out

    return window


def collect_into(size, gcore_ref, grow_ref, gcol_ref, gcorner_ref, cols, row_mask):
    half, at, lanes, boundary = common(size)

    def collect(start, k, quads):
        for r in range(2):
            side = jnp.where(cols[0], jnp.where(cols[1], 0.0, quads[r][1]), quads[r][0])
            own = [jnp.where(cols[c], quads[r][c], 0.0) for c in range(2)]
            if boundary(r, start):
                mask = row_mask(r, start)
                for c in range(2):
                    gcore_ref[k, at(r, start), lanes(c)] += jnp.where(mask, own[c], 0.0)
                    grow_ref[k, pl.ds(start, CHUNK), lanes(c)] += jnp.where(mask, 0.0, own[c])
                gcol_ref[k, at(r, start), :] += jnp.where(mask, side, 0.0)
                gcorner_ref[k, pl.ds(start, CHUNK), :] += jnp.where(mask, 0.0, side)
            else:
                for c in range(2):
                    gcore_ref[k, at(r, start), lanes(c)] += own[c]
                gcol_ref[k, at(r, start), :] += side

    return collect


TILE = 8


def roller(size, shift_row, shift_col, twice_ref):
    half = size // 2
    lane = lax.broadcasted_iota(jnp.int32, (TILE, half), 1)
    far = (shift_col >= half).astype(jnp.int32)
    step = shift_col - far * half
    other = (lane < step).astype(jnp.int32) != far
    whole = shift_row // TILE
    rest = shift_row - whole * TILE
    row = lax.broadcasted_iota(jnp.int32, (CHUNK, size), 0)
    early = lax.rem(row, TILE) < rest

    def put(k, start, low, high):
        low, high = pltpu.roll(low, step, 1), pltpu.roll(high, step, 1)
        turned = (jnp.where(other, high, low), jnp.where(other, low, high))
        for c in range(2):
            value = pltpu.roll(turned[c], rest, 0)
            twice_ref[k, start : start + TILE, c * half : (c + 1) * half] = value

    def take(k, start):
        tiles = [
            pl.multiple_of(lax.rem(size + start + step * TILE - whole * TILE, size), TILE)
            for step in range(-1, CHUNK // TILE)
        ]
        rows = jnp.concatenate([twice_ref[k, pl.ds(tile, TILE), :] for tile in tiles], axis=0)
        return jnp.where(early, rows[:CHUNK], rows[TILE:])

    return put, take


def shifts(size, top, lead):
    return lax.rem(top + (size - MARGIN), size), lax.rem(lead + (size - MARGIN), size)


def grad_kernel(
    count_ref, offset_ref, core_ref, row_ref, col_ref, corner_ref, probe_ref, measured_ref, table_ref,
    gcore_ref, grow_ref, gcol_ref, gcorner_ref, gprobe_ref, *scratch,
):
    size = probe_ref.shape[1]
    half, at, lanes, _ = common(size)
    sets = [scratch[: len(scratch) // 2], scratch[len(scratch) // 2 :]]
    for ref in (gcore_ref, grow_ref, gcol_ref, gcorner_ref, gprobe_ref):
        ref[...] = jnp.zeros_like(ref)

    def position(slot, valid, window_ref, moved_ref, rolled_ref, twice_ref, *work):
        put, right, left, take = stages(size, table_ref, *work)
        found = []
        stage = found.append
        top, lead = offset_ref[slot, 0], offset_ref[slot, 1]
        shift_row, shift_col = shifts(size, top, lead)
        cols, row_mask = masks(size, top, lead)
        window = window_of(size, core_ref, row_ref, col_ref, corner_ref, cols, row_mask)
        collect = collect_into(size, gcore_ref, grow_ref, gcol_ref, gcorner_ref, cols, row_mask)
        roll_put, roll_take = roller(size, shift_row, shift_col, twice_ref)

        def part_1():
            for k in range(2):
                for start in range(0, size, TILE):
                    roll_put(k, start, *[probe_ref[k, pl.ds(start, TILE), lanes(c)] for c in range(2)])
            for start in range(0, half, CHUNK):
                one_real, one_imag = window(start, 0), window(start, 1)
                real, imag = empty(), empty()
                for r in range(2):
                    turned = [roll_take(k, r * half + start) for k in range(2)]
                    for c in range(2):
                        pr, pi = [t[:, c * half : (c + 1) * half] for t in turned]
                        wr, wi = one_real[r][c], one_imag[r][c]
                        rolled_ref[0, at(r, start), lanes(c)] = pr
                        rolled_ref[1, at(r, start), lanes(c)] = pi
                        window_ref[0, at(r, start), lanes(c)] = wr
                        window_ref[1, at(r, start), lanes(c)] = wi
                        real[r][c] = pr * wr - pi * wi
                        imag[r][c] = pr * wi + pi * wr
                put(start, fold(real), fold(imag))
        stage(part_1)

        stage(lambda: right(0, 1))
        stage(lambda: left(0, 1))
        def part_2():
            for start in range(0, half, CHUNK):
                moved_real, moved_imag = fold(take(start, 0)), fold(take(start, 1))
                two_real, two_imag = window(start, 2), window(start, 3)
                real, imag = empty(), empty()
                for r in range(2):
                    for c in range(2):
                        mr, mi = moved_real[r][c], moved_imag[r][c]
                        tr, ti = two_real[r][c], two_imag[r][c]
                        moved_ref[0, at(r, start), lanes(c)] = mr
                        moved_ref[1, at(r, start), lanes(c)] = mi
                        window_ref[2, at(r, start), lanes(c)] = tr
                        window_ref[3, at(r, start), lanes(c)] = ti
                        real[r][c] = mr * tr - mi * ti
                        imag[r][c] = mr * ti + mi * tr
                put(start, fold(real), fold(imag))
        stage(part_2)

        stage(lambda: right(1, 1))
        stage(lambda: left(1, 1))
        def part_3():
            for start in range(0, half, CHUNK):
                far_real, far_imag = take(start, 0), take(start, 1)
                real, imag = empty(), empty()
                for p in range(2):
                    for q in range(2):
                        fr, fi = far_real[p][q], far_imag[p][q]
                        misfit = fr * fr + fi * fi - measured_ref[slot, at(p, start), lanes(q)]
                        if valid is not None:
                            misfit = jnp.where(valid, misfit, 0.0)
                        real[p][q] = misfit * fr
                        imag[p][q] = misfit * fi
                put(start, real, imag)
        stage(part_3)

        stage(lambda: right(1, 0))
        stage(lambda: left(1, 0))
        def part_4():
            for start in range(0, half, CHUNK):
                back_real, back_imag = fold(take(start, 0)), fold(take(start, 1))
                real, imag, two_real, two_imag = empty(), empty(), empty(), empty()
                for r in range(2):
                    for c in range(2):
                        br, bi = back_real[r][c], back_imag[r][c]
                        mr, mi = [moved_ref[k, at(r, start), lanes(c)] for k in range(2)]
                        tr, ti = [window_ref[k, at(r, start), lanes(c)] for k in (2, 3)]
                        two_real[r][c] = mr * br + mi * bi
                        two_imag[r][c] = mr * bi - mi * br
                        real[r][c] = tr * br + ti * bi
                        imag[r][c] = tr * bi - ti * br
                put(start, fold(real), fold(imag))
                collect(start, 2, two_real)
                collect(start, 3, two_imag)
        stage(part_4)

        stage(lambda: right(0, 0))
        stage(lambda: left(0, 0))
        def part_5():
            roll_put, roll_take = roller(
                size, lax.rem(size - shift_row, size), lax.rem(size - shift_col, size), twice_ref
            )
            for start in range(0, half, CHUNK):
                wave_real, wave_imag = fold(take(start, 0)), fold(take(start, 1))
                one_real, one_imag = empty(), empty()
                for r in range(2):
                    turned = empty()
                    for c in range(2):
                        wr, wi = wave_real[r][c], wave_imag[r][c]
                        pr, pi = [rolled_ref[k, at(r, start), lanes(c)] for k in range(2)]
                        fr, fi = [window_ref[k, at(r, start), lanes(c)] for k in range(2)]
                        one_real[r][c] = pr * wr + pi * wi
                        one_imag[r][c] = pr * wi - pi * wr
                        turned[0][c] = fr * wr + fi * wi
                        turned[1][c] = fr * wi - fi * wr
                    for k in range(2):
                        for tile in range(0, CHUNK, TILE):
                            roll_put(k, r * half + start + tile, *[t[tile : tile + TILE] for t in turned[k]])
                collect(start, 0, one_real)
                collect(start, 1, one_imag)
            for k in range(2):
                for start in range(0, size, CHUNK):
                    gprobe_ref[k, start : start + CHUNK, :] += roll_take(k, start)

        stage(part_5)

        return found

    def visit(pair, carry):
        last = count_ref[0] - 1
        slots = (2 * pair, jnp.minimum(2 * pair + 1, last))
        valid = (None, 2 * pair + 1 <= last)
        each = [position(s, v, *refs) for s, v, refs in zip(slots, valid, sets)]
        for step in range(len(each[0]) + SKEW):
            if step < len(each[0]):
                each[0][step]()
            if step >= SKEW:
                each[1][step - SKEW]()
        return carry

    lax.fori_loop(0, (count_ref[0] + 1) // 2, visit, 0)


def sort_measured(count, values, order):
    return pl.pallas_call(
        sort_kernel,
        out_shape=jax.ShapeDtypeStruct(values.shape, values.dtype),
        in_specs=[pl.BlockSpec(memory_space=pltpu.SMEM)] + [pl.BlockSpec(memory_space=pltpu.VMEM)] * 2,
        out_specs=pl.BlockSpec(memory_space=pltpu.VMEM),
        compiler_params=pltpu.CompilerParams(vmem_limit_bytes=24 * 1024 * 1024),
        name="sort_measured",
    )(count, values, order)


def call(kernel, name, inputs, scalars, outputs, scratch, size, products):
    f32, bf16 = jnp.float32, jnp.bfloat16
    vmem = pl.BlockSpec(memory_space=pltpu.VMEM)
    work = [pltpu.VMEM((2, size, size), bf16)] * 4 + [pltpu.VMEM((2, size, size), f32)] * 2
    return pl.pallas_call(
        kernel,
        out_shape=[jax.ShapeDtypeStruct(s, f32) for s in outputs],
        in_specs=[pl.BlockSpec(memory_space=pltpu.SMEM)] * scalars + [vmem] * (len(inputs) - scalars),
        out_specs=[vmem] * len(outputs),
        scratch_shapes=([pltpu.VMEM(s, f32) for s in scratch] + work) * 2,
        compiler_params=pltpu.CompilerParams(vmem_limit_bytes=24 * 1024 * 1024),
        cost_estimate=pl.CostEstimate(
            flops=products * 2 * size**3, transcendentals=0, bytes_accessed=sum(x.size * 4 for x in inputs)
        ),
        name=name,
    )(*inputs)


def shifted(value, axis, step):
    count = lax.axis_size(axis)
    return lax.ppermute(value, axis, [(i, (i + step) % count) for i in range(count)])


def pack(value):
    rows = value.shape[1] // 2
    return jnp.concatenate([value[:, :rows], value[:, rows:]], axis=2)


def unpack(from_right, from_left):
    parts_of = [
        jnp.concatenate([from_right[..., s], from_left[..., s]], axis=2)
        for s in (slice(0, MARGIN), slice(MARGIN, None))
    ]
    return jnp.concatenate(parts_of, axis=1)


def swap_cols(to_left, to_right):
    return unpack(shifted(pack(to_left), "tx", -1), shifted(pack(to_right), "tx", 1))


def sides(core):
    size = core.shape[1]
    from_below = shifted(core[:, :MARGIN], "ty", -1)
    from_above = shifted(core[:, size - MARGIN :], "ty", 1)
    col = swap_cols(core[:, :, :MARGIN], core[:, :, size - MARGIN :])
    return jnp.concatenate([from_below, from_above], axis=1), col


def corners(row):
    return swap_cols(row[:, :, :MARGIN], row[:, :, row.shape[2] - MARGIN :])


def owned_cols(side):
    from_left = shifted(pack(side[:, :, :MARGIN]), "tx", 1)
    from_right = shifted(pack(side[:, :, MARGIN:]), "tx", -1)
    return unpack(from_left, from_right)


def owned_rows(side):
    return shifted(side[:, :MARGIN], "ty", 1), shifted(side[:, MARGIN:], "ty", -1)


def spread_cols(side, size):
    gap = jnp.zeros(side.shape[:2] + (size - 2 * MARGIN,), side.dtype)
    return jnp.concatenate([side[:, :, :MARGIN], gap, side[:, :, MARGIN:]], axis=2)


def spread_rows(low, high, size):
    gap = jnp.zeros((low.shape[0], size - 2 * MARGIN, low.shape[2]), low.dtype)
    return jnp.concatenate([low, gap, high], axis=1)


def split(count, inner):
    found = []
    while inner < count:
        members = 4 if (count // inner) % 4 == 0 else 2
        found.append((inner, members))
        inner *= members
    return found


def ring(axis, inner, members, step):
    count = lax.axis_size(axis)
    pairs = []
    for i in range(count):
        low, mid, high = i % inner, (i // inner) % members, i // (inner * members)
        pairs.append((i, (high * members + (mid + step) % members) * inner + low))
    return pairs


def place(axis, inner, members):
    return (lax.axis_index(axis) // inner) % members


def scatter_round(value, axis, inner, members):
    pieces = value.reshape((members, value.shape[0] // members) + value.shape[1:])
    me = place(axis, inner, members)
    pick = lambda step: lax.dynamic_index_in_dim(pieces, (me + step) % members, 0, keepdims=False)
    out = pick(0)
    for got in [lax.ppermute(pick(s), axis, ring(axis, inner, members, s)) for s in range(1, members)]:
        out = out + got
    return out


def gather_round(value, axis, inner, members):
    me = place(axis, inner, members)
    got = [value] + [lax.ppermute(value, axis, ring(axis, inner, members, s)) for s in range(1, members)]
    out = jnp.zeros((members,) + value.shape, value.dtype)
    for step, piece in enumerate(got):
        out = lax.dynamic_update_index_in_dim(out, piece, (me + members - step) % members, 0)
    return out.reshape((members * value.shape[0],) + value.shape[1:])


def exchange_round(value, axis, inner, members):
    out = value
    for got in [lax.ppermute(value, axis, ring(axis, inner, members, s)) for s in range(1, members)]:
        out = out + got
    return out


def total_over_devices(value):
    flat = value.reshape(value.shape[0] * value.shape[1], value.shape[2])
    steps = [("tx", 1, 2)] + [("ty", *s) for s in split(lax.axis_size("ty"), 1)]
    for each in steps:
        flat = scatter_round(flat, *each)
    for each in split(lax.axis_size("tx"), 2):
        flat = exchange_round(flat, "tx", *each)
    for each in reversed(steps):
        flat = gather_round(flat, *each)
    return flat.reshape(value.shape)


def make_body(table, order):
    def body(object_slices, probe, position_count, offsets, intensities):
        size = probe.shape[1]
        devices = lax.axis_size("ty") * lax.axis_size("tx")
        count = position_count.reshape(1)
        place_of = offsets.reshape(offsets.shape[2:])
        core = object_slices.reshape((4,) + object_slices.shape[2:])
        measured = sort_measured(count, intensities.reshape(intensities.shape[2:]), order)
        row, col = sides(core)
        for step in range(ITERS):
            inputs = (count, place_of, core, row, col, corners(row), probe, measured, table)
            plane, field = (2, size, size), (4, size, size)
            gcore, grow, gcol, gcorner, gprobe = call(
                grad_kernel, "gradients", inputs, 2, [x.shape for x in inputs[2:7]],
                [field, plane, plane, (2, size, size)], size, 240,
            )
            peak = jnp.max(probe[0] * probe[0] + probe[1] * probe[1]) + 1e-06
            low, high = owned_rows(grow + spread_cols(owned_cols(gcorner), size))
            total = gcore + spread_cols(owned_cols(gcol), size) + spread_rows(low, high, size)
            core = core - object_rate / peak * total
            summed = total_over_devices(gprobe)
            if step + 1 < ITERS:
                row, col = sides(core)
            probe = probe - probe_rate / devices * summed
        return core.reshape(object_slices.shape), probe

    return body


def solution(mesh):
    size = 256
    table, order = tables(size), lane_order(size)

    def run(object_slices, probe, position_count, offsets, intensities):
        placed = (
            P(None, None, "ty", "tx"),
            P(),
            P("ty", "tx"),
            P("ty", "tx", None, None),
            P("ty", "tx", None, None, None),
        )
        return jax.shard_map(
            make_body(jnp.asarray(table), jnp.asarray(order)),
            mesh=mesh,
            in_specs=placed,
            out_specs=(P(None, None, "ty", "tx"), P()),
            check_vma=False,
        )(object_slices, probe, position_count, offsets, intensities)

    return run
```

profile of v0, /device:TPU:0, one launch (start us, length us, event | category | flops | bytes accessed | tf_op | source)
XLA Modules:
  0.0 165.0 jit_solution(16628080728208333222)
XLA Ops:
  0.6 1.9 %fusion.15 = (f32[4,64,256]{2,1,0:T(8,128)S(1)}, f32[4,64,256]{2,1,0:T(8,128)}) fusion(f32[4,256,256]{2,1,0:T(8,128)} %bitcast.71), kind=kLoop, calls=%fused_computation.76 | loop fusion | bytes 1048576 | tf_op jit(solution)/shard_map/slice | solution.py:430
  2.5 3.9 %collective-permute-start = (f32[4,64,256]{2,1,0:T(8,128)S(1)}, f32[4,64,256]{2,1,0:T(8,128)S(1)}, u32[]{:S(2)}, u32[]{:S(2)}) collective-permute-start(f32[4,64,256]{2,1,0:T(8,128)S(1)} %get-tuple-element.36), channel_id=1, source_target_pairs={{0,24},{8,0},{16,8},{24,16},{1,25},{9,1},{17,9},{25,17},{2,26},{10... | collective-permute-start | bytes 786440 | tf_op jit(solution)/shard_map/ppermute | solution.py:408
  7.5 2.8 %collective-permute-start.2 = (f32[4,128,128]{2,1,0:T(8,128)}, f32[4,128,128]{2,1,0:T(8,128)S(1)}, u32[]{:S(2)}, u32[]{:S(2)}) collective-permute-start(f32[4,128,128]{2,1,0:T(8,128)} %pad_maximum_fusion.2), channel_id=1, source_target_pairs={{0,7},{1,0},{2,1},{3,2},{4,3},{5,4},{6,5},{7,6},{8,15},{9,8},{10,9... | collective-permute-start | bytes 786440 | tf_op jit(solution)/shard_map/ppermute | solution.py:408
  14.7 2.8 %sort_measured.1.measured_ref = f32[5,256,256]{2,1,0:T(8,128)S(1)} custom-call(s32[1]{0:T(128)} %bitcast.68.count_ref, f32[5,256,256]{2,1,0:T(8,128)S(1)} %bitcast.74, bf16[2,256,256]{2,1,0:T(8,128)(2,1)S(1)} %copy-done.6), custom_call_target="tpu_custom_call" | custom-call | tf_op jit(solution)/shard_map/sort_measured/pallas_call | solution.py:378
  18.8 2.2 %collective-permute-start.4 = (f32[4,64,128]{2,1,0:T(8,128)S(1)}, f32[4,64,128]{2,1,0:T(8,128)S(1)}, u32[]{:S(2)}, u32[]{:S(2)}) collective-permute-start(f32[4,64,128]{2,1,0:T(8,128)S(1)} %pad_maximum_fusion.10), channel_id=1, source_target_pairs={{0,7},{1,0},{2,1},{3,2},{4,3},{5,4},{6,5},{7,6},{8,15},{9,8},{10,9... | collective-permute-start | bytes 393224 | tf_op jit(solution)/shard_map/ppermute | solution.py:408
  21.8 2.1 %collective-permute-done.4 = f32[4,64,128]{2,1,0:T(8,128)S(1)} collective-permute-done((f32[4,64,128]{2,1,0:T(8,128)S(1)}, f32[4,64,128]{2,1,0:T(8,128)S(1)}, u32[]{:S(2)}, u32[]{:S(2)}) %collective-permute-start.4) | collective-permute-done | bytes 131104 | tf_op jit(solution)/shard_map/ppermute | solution.py:408
  24.0 3.4 %collective-permute-done.5 = f32[4,64,128]{2,1,0:T(8,128)S(1)} collective-permute-done((f32[4,64,128]{2,1,0:T(8,128)S(1)}, f32[4,64,128]{2,1,0:T(8,128)S(1)}, u32[]{:S(2)}, u32[]{:S(2)}) %collective-permute-start.5) | collective-permute-done | bytes 131104 | tf_op jit(solution)/shard_map/ppermute | solution.py:408
  27.7 13.1 %gradients.2 = (f32[4,256,256]{2,1,0:T(8,128)S(1)}, f32[4,128,256]{2,1,0:T(8,128)S(1)}, f32[4,256,128]{2,1,0:T(8,128)S(1)}, f32[4,128,128]{2,1,0:T(8,128)S(1)}, f32[2,256,256]{2,1,0:T(8,128)S(1)}) custom-call(s32[1]{0:T(128)} %bitcast.69.count_ref, s32[5,2]{1,0:T(8,128)S(1)} %copy.9.offset_ref, f32[4,256,256]{2,1,0:T(8,128)S(1)} %bitcast.73, ...), custom_call_target="tpu_custom_call" | custom-call | flops 8053063680 | bytes 8388652 | tf_op jit(solution)/shard_map/gradients/pallas_call | solution.py:392
  41.8 3.1 %collective-permute-start.9 = (f32[4,64,128]{2,1,0:T(8,128)S(1)}, f32[4,64,128]{2,1,0:T(8,128)S(1)}, u32[]{:S(2)}, u32[]{:S(2)}) collective-permute-start(f32[4,64,128]{2,1,0:T(8,128)S(1)} %pad_maximum_fusion.13), channel_id=1, source_target_pairs={{0,7},{1,0},{2,1},{3,2},{4,3},{5,4},{6,5},{7,6},{8,15},{9,8},{10,9... | collective-permute-start | bytes 393224 | tf_op jit(solution)/shard_map/ppermute | solution.py:408
  45.5 3.6 %collective-permute-start.7 = (f32[4,128,128]{2,1,0:T(8,128)S(1)}, f32[4,128,128]{2,1,0:T(8,128)S(1)}, u32[]{:S(2)}, u32[]{:S(2)}) collective-permute-start(f32[4,128,128]{2,1,0:T(8,128)S(1)} %pad_maximum_fusion.5), channel_id=1, source_target_pairs={{0,7},{1,0},{2,1},{3,2},{4,3},{5,4},{6,5},{7,6},{8,15},{9,8},{10,9... | collective-permute-start | bytes 786440 | tf_op jit(solution)/shard_map/ppermute | solution.py:408
  49.7 5.3 %collective-permute-start.10 = (f32[4,64,256]{2,1,0:T(8,128)S(1)}, f32[4,64,256]{2,1,0:T(8,128)S(1)}, u32[]{:S(2)}, u32[]{:S(2)}) collective-permute-start(f32[4,64,256]{2,1,0:T(8,128)S(1)} %get-tuple-element.46), channel_id=1, source_target_pairs={{0,8},{8,16},{16,24},{24,0},{1,9},{9,17},{17,25},{25,1},{2,10},{10... | collective-permute-start | bytes 786440 | tf_op jit(solution)/shard_map/ppermute | solution.py:408
  55.1 2.1 %collective-permute-start.13 = (f32[64,256]{1,0:T(8,128)S(1)}, f32[64,256]{1,0:T(8,128)S(1)}, u32[]{:S(2)}, u32[]{:S(2)}) collective-permute-start(f32[64,256]{1,0:T(8,128)S(1)} %get-tuple-element.67), channel_id=1, source_target_pairs={{0,8},{8,16},{16,24},{24,0},{1,9},{9,17},{17,25},{25,1},{2,10},{10... | collective-permute-start | bytes 196616 | tf_op jit(solution)/shard_map/ppermute | solution.py:487
  57.8 4.0 %collective-permute-start.15 = (f32[64,256]{1,0:T(8,128)S(1)}, f32[64,256]{1,0:T(8,128)S(1)}, u32[]{:S(2)}, u32[]{:S(2)}) collective-permute-start(f32[64,256]{1,0:T(8,128)S(1)} %get-tuple-element.68), channel_id=1, source_target_pairs={{0,24},{8,0},{16,8},{24,16},{1,25},{9,1},{17,9},{25,17},{2,26},{10... | collective-permute-start | bytes 196616 | tf_op jit(solution)/shard_map/ppermute | solution.py:487
  62.2 5.5 %collective-permute-done.13 = f32[64,256]{1,0:T(8,128)S(1)} collective-permute-done((f32[64,256]{1,0:T(8,128)S(1)}, f32[64,256]{1,0:T(8,128)S(1)}, u32[]{:S(2)}, u32[]{:S(2)}) %collective-permute-start.13) | collective-permute-done | bytes 65568 | tf_op jit(solution)/shard_map/ppermute | solution.py:487
  67.8 3.4 %collective-permute-start.17 = (f32[64,256]{1,0:T(8,128)S(1)}, f32[64,256]{1,0:T(8,128)S(1)}, u32[]{:S(2)}, u32[]{:S(2)}) collective-permute-start(f32[64,256]{1,0:T(8,128)S(1)} %fusion.11), channel_id=1, source_target_pairs={{0,4},{1,5},{2,6},{3,7},{4,0},{5,1},{6,2},{7,3},{8,12},{9,13},{10,... | collective-permute-start | bytes 196616 | tf_op jit(solution)/shard_map/ppermute | solution.py:503
  71.1 2.8 %collective-permute-start.18 = (f32[64,256]{1,0:T(8,128)S(1)}, f32[64,256]{1,0:T(8,128)S(1)}, u32[]{:S(2)}, u32[]{:S(2)}) collective-permute-start(f32[64,256]{1,0:T(8,128)S(1)} %fusion.11), channel_id=1, source_target_pairs={{0,6},{1,7},{2,0},{3,1},{4,2},{5,3},{6,4},{7,5},{8,14},{9,15},{10,... | collective-permute-start | bytes 196616 | tf_op jit(solution)/shard_map/ppermute | solution.py:503
  76.2 2.1 %collective-permute-start.19 = (f32[64,256]{1,0:T(8,128)S(1)}, f32[64,256]{1,0:T(8,128)S(1)}, u32[]{:S(2)}, u32[]{:S(2)}) collective-permute-start(f32[64,256]{1,0:T(8,128)S(1)} %get-tuple-element.25), channel_id=1, source_target_pairs={{0,8},{8,16},{16,24},{24,0},{1,9},{9,17},{17,25},{25,1},{2,10},{10... | collective-permute-start | bytes 196616 | tf_op jit(solution)/shard_map/ppermute | solution.py:494
  85.3 5.2 %collective-permute-done.23 = f32[4,64,256]{2,1,0:T(8,128)S(1)} collective-permute-done((f32[4,64,256]{2,1,0:T(8,128)S(1)}, f32[4,64,256]{2,1,0:T(8,128)S(1)}, u32[]{:S(2)}, u32[]{:S(2)}) %collective-permute-start.23) | collective-permute-done | bytes 262176 | tf_op jit(solution)/shard_map/ppermute | solution.py:408
  90.6 4.7 %collective-permute-done.24 = f32[4,64,256]{2,1,0:T(8,128)S(1)} collective-permute-done((f32[4,64,256]{2,1,0:T(8,128)S(1)}, f32[4,64,256]{2,1,0:T(8,128)S(1)}, u32[]{:S(2)}, u32[]{:S(2)}) %collective-permute-start.24) | collective-permute-done | bytes 262176 | tf_op jit(solution)/shard_map/ppermute | solution.py:408
  100.3 3.1 %collective-permute-done.28 = f32[4,64,128]{2,1,0:T(8,128)} collective-permute-done((f32[4,64,128]{2,1,0:T(8,128)}, f32[4,64,128]{2,1,0:T(8,128)}, u32[]{:S(2)}, u32[]{:S(2)}) %collective-permute-start.28) | collective-permute-done | bytes 131104 | tf_op jit(solution)/shard_map/ppermute | solution.py:408
  106.2 12.8 %gradients.3 = (f32[4,256,256]{2,1,0:T(8,128)S(1)}, f32[4,128,256]{2,1,0:T(8,128)S(1)}, f32[4,256,128]{2,1,0:T(8,128)S(1)}, f32[4,128,128]{2,1,0:T(8,128)S(1)}, f32[2,256,256]{2,1,0:T(8,128)S(1)}) custom-call(s32[1]{0:T(128)} %bitcast.70.count_ref, s32[5,2]{1,0:T(8,128)S(1)} %copy.9.offset_ref, f32[4,256,256]{2,1,0:T(8,128)S(1)} %fusion.2.core_ref, ...), custom_call_target="tpu_custom_call" | custom-call | flops 8053063680 | bytes 8388652 | tf_op jit(solution)/shard_map/gradients/pallas_call | solution.py:392
  120.1 3.1 %collective-permute-start.32 = (f32[4,64,128]{2,1,0:T(8,128)S(1)}, f32[4,64,128]{2,1,0:T(8,128)S(1)}, u32[]{:S(2)}, u32[]{:S(2)}) collective-permute-start(f32[4,64,128]{2,1,0:T(8,128)S(1)} %pad_maximum_fusion.17), channel_id=1, source_target_pairs={{0,7},{1,0},{2,1},{3,2},{4,3},{5,4},{6,5},{7,6},{8,15},{9,8},{10,9... | collective-permute-start | bytes 393224 | tf_op jit(solution)/shard_map/ppermute | solution.py:408
  123.7 3.6 %collective-permute-start.30 = (f32[4,128,128]{2,1,0:T(8,128)S(1)}, f32[4,128,128]{2,1,0:T(8,128)S(1)}, u32[]{:S(2)}, u32[]{:S(2)}) collective-permute-start(f32[4,128,128]{2,1,0:T(8,128)S(1)} %pad_maximum_fusion.9), channel_id=1, source_target_pairs={{0,7},{1,0},{2,1},{3,2},{4,3},{5,4},{6,5},{7,6},{8,15},{9,8},{10,9... | collective-permute-start | bytes 786440 | tf_op jit(solution)/shard_map/ppermute | solution.py:408
  128.0 3.4 %collective-permute-start.33 = (f32[4,64,256]{2,1,0:T(8,128)S(1)}, f32[4,64,256]{2,1,0:T(8,128)S(1)}, u32[]{:S(2)}, u32[]{:S(2)}) collective-permute-start(f32[4,64,256]{2,1,0:T(8,128)S(1)} %get-tuple-element.38), channel_id=1, source_target_pairs={{0,8},{8,16},{16,24},{24,0},{1,9},{9,17},{17,25},{25,1},{2,10},{10... | collective-permute-start | bytes 786440 | tf_op jit(solution)/shard_map/ppermute | solution.py:408
  131.4 2.5 %collective-permute-start.34 = (f32[4,64,256]{2,1,0:T(8,128)S(1)}, f32[4,64,256]{2,1,0:T(8,128)S(1)}, u32[]{:S(2)}, u32[]{:S(2)}) collective-permute-start(f32[4,64,256]{2,1,0:T(8,128)S(1)} %get-tuple-element.39), channel_id=1, source_target_pairs={{0,24},{8,0},{16,8},{24,16},{1,25},{9,1},{17,9},{25,17},{2,26},{10... | collective-permute-start | bytes 786440 | tf_op jit(solution)/shard_map/ppermute | solution.py:408
  134.0 2.5 %collective-permute-start.37 = (f32[64,256]{1,0:T(8,128)S(1)}, f32[64,256]{1,0:T(8,128)S(1)}, u32[]{:S(2)}, u32[]{:S(2)}) collective-permute-start(f32[64,256]{1,0:T(8,128)S(1)} %get-tuple-element.56), channel_id=1, source_target_pairs={{0,16},{8,24},{16,0},{24,8},{1,17},{9,25},{17,1},{25,9},{2,18},{10... | collective-permute-start | bytes 196616 | tf_op jit(solution)/shard_map/ppermute | solution.py:487
  136.6 2.9 %collective-permute-start.38 = (f32[64,256]{1,0:T(8,128)S(1)}, f32[64,256]{1,0:T(8,128)S(1)}, u32[]{:S(2)}, u32[]{:S(2)}) collective-permute-start(f32[64,256]{1,0:T(8,128)S(1)} %get-tuple-element.55), channel_id=1, source_target_pairs={{0,24},{8,0},{16,8},{24,16},{1,25},{9,1},{17,9},{25,17},{2,26},{10... | collective-permute-start | bytes 196616 | tf_op jit(solution)/shard_map/ppermute | solution.py:487
  139.7 7.8 %collective-permute-done.36 = f32[64,256]{1,0:T(8,128)S(1)} collective-permute-done((f32[64,256]{1,0:T(8,128)S(1)}, f32[64,256]{1,0:T(8,128)S(1)}, u32[]{:S(2)}, u32[]{:S(2)}) %collective-permute-start.36) | collective-permute-done | bytes 65568 | tf_op jit(solution)/shard_map/ppermute | solution.py:487
  147.6 2.4 %collective-permute-start.40 = (f32[64,256]{1,0:T(8,128)S(1)}, f32[64,256]{1,0:T(8,128)S(1)}, u32[]{:S(2)}, u32[]{:S(2)}) collective-permute-start(f32[64,256]{1,0:T(8,128)S(1)} %fusion.9), channel_id=1, source_target_pairs={{0,4},{1,5},{2,6},{3,7},{4,0},{5,1},{6,2},{7,3},{8,12},{9,13},{10,... | collective-permute-start | bytes 196616 | tf_op jit(solution)/shard_map/ppermute | solution.py:503
  150.0 2.8 %collective-permute-start.41 = (f32[64,256]{1,0:T(8,128)S(1)}, f32[64,256]{1,0:T(8,128)S(1)}, u32[]{:S(2)}, u32[]{:S(2)}) collective-permute-start(f32[64,256]{1,0:T(8,128)S(1)} %fusion.9), channel_id=1, source_target_pairs={{0,6},{1,7},{2,0},{3,1},{4,2},{5,3},{6,4},{7,5},{8,14},{9,15},{10,... | collective-permute-start | bytes 196616 | tf_op jit(solution)/shard_map/ppermute | solution.py:503
  155.0 2.9 %collective-permute-start.42 = (f32[64,256]{1,0:T(8,128)S(1)}, f32[64,256]{1,0:T(8,128)S(1)}, u32[]{:S(2)}, u32[]{:S(2)}) collective-permute-start(f32[64,256]{1,0:T(8,128)S(1)} %get-tuple-element.23), channel_id=1, source_target_pairs={{0,8},{8,16},{16,24},{24,0},{1,9},{9,17},{17,25},{25,1},{2,10},{10... | collective-permute-start | bytes 196616 | tf_op jit(solution)/shard_map/ppermute | solution.py:494
  158.2 1.9 %collective-permute-start.44 = (f32[64,256]{1,0:T(8,128)S(1)}, f32[64,256]{1,0:T(8,128)S(1)}, u32[]{:S(2)}, u32[]{:S(2)}) collective-permute-start(f32[64,256]{1,0:T(8,128)S(1)} %get-tuple-element.23), channel_id=1, source_target_pairs={{0,24},{8,0},{16,8},{24,16},{1,25},{9,1},{17,9},{25,17},{2,26},{10... | collective-permute-start | bytes 196616 | tf_op jit(solution)/shard_map/ppermute | solution.py:494
  (178 shorter events, 35.8 us)
Async XLA Ops:
  2.5 15.0 %collective-permute-start = (f32[4,64,256]{2,1,0:T(8,128)S(1)}, f32[4,64,256]{2,1,0:T(8,128)S(1)}, u32[]{:S(2)}, u32[]{:S(2)}) collective-permute-start(f32[4,64,256]{2,1,0:T(8,128)S(1)} %get-tuple-element.36), channel_id=1, source_target_pairs={{0,24},{8,0},{16,8},{24,16},{1,25},{9,1},{17,9},{25,17},{2,26},{10... | collective-permute-start | bytes 786440 | tf_op jit(solution)/shard_map/ppermute | solution.py:408
  6.4 12.2 %collective-permute-start.1 = (f32[4,64,256]{2,1,0:T(8,128)}, f32[4,64,256]{2,1,0:T(8,128)S(1)}, u32[]{:S(2)}, u32[]{:S(2)}) collective-permute-start(f32[4,64,256]{2,1,0:T(8,128)} %get-tuple-element.37), channel_id=1, source_target_pairs={{0,8},{8,16},{16,24},{24,0},{1,9},{9,17},{17,25},{25,1},{2,10},{10... | collective-permute-start | bytes 786440 | tf_op jit(solution)/shard_map/ppermute | solution.py:408
  7.5 13.7 %collective-permute-start.2 = (f32[4,128,128]{2,1,0:T(8,128)}, f32[4,128,128]{2,1,0:T(8,128)S(1)}, u32[]{:S(2)}, u32[]{:S(2)}) collective-permute-start(f32[4,128,128]{2,1,0:T(8,128)} %pad_maximum_fusion.2), channel_id=1, source_target_pairs={{0,7},{1,0},{2,1},{3,2},{4,3},{5,4},{6,5},{7,6},{8,15},{9,8},{10,9... | collective-permute-start | bytes 786440 | tf_op jit(solution)/shard_map/ppermute | solution.py:408
  11.1 10.3 %collective-permute-start.3 = (f32[4,128,128]{2,1,0:T(8,128)}, f32[4,128,128]{2,1,0:T(8,128)S(1)}, u32[]{:S(2)}, u32[]{:S(2)}) collective-permute-start(f32[4,128,128]{2,1,0:T(8,128)} %pad_maximum_fusion.3), channel_id=1, source_target_pairs={{0,1},{1,2},{2,3},{3,4},{4,5},{5,6},{6,7},{7,0},{8,9},{9,10},{10,1... | collective-permute-start | bytes 786440 | tf_op jit(solution)/shard_map/ppermute | solution.py:408
  40.8 14.2 %collective-permute-start.12 = (f32[256,256]{1,0:T(8,128)S(1)}, f32[256,256]{1,0:T(8,128)S(1)}, u32[]{:S(2)}, u32[]{:S(2)}) collective-permute-start(f32[256,256]{1,0:T(8,128)S(1)} %dynamic-slice_bitcast_fusion.1), channel_id=1, source_target_pairs={{0,1},{1,0},{2,3},{3,2},{4,5},{5,4},{6,7},{7,6},{8,9},{9,8},{10,11... | collective-permute-start | bytes 786440 | tf_op jit(solution)/shard_map/ppermute | solution.py:487
  41.1 7.9 %collective-permute-start.8 = (f32[4,64,128]{2,1,0:T(8,128)S(1)}, f32[4,64,128]{2,1,0:T(8,128)S(1)}, u32[]{:S(2)}, u32[]{:S(2)}) collective-permute-start(f32[4,64,128]{2,1,0:T(8,128)S(1)} %pad_maximum_fusion.12), channel_id=1, source_target_pairs={{0,1},{1,2},{2,3},{3,4},{4,5},{5,6},{6,7},{7,0},{8,9},{9,10},{10,1... | collective-permute-start | bytes 393224 | tf_op jit(solution)/shard_map/ppermute | solution.py:408
  41.8 7.3 %collective-permute-start.9 = (f32[4,64,128]{2,1,0:T(8,128)S(1)}, f32[4,64,128]{2,1,0:T(8,128)S(1)}, u32[]{:S(2)}, u32[]{:S(2)}) collective-permute-start(f32[4,64,128]{2,1,0:T(8,128)S(1)} %pad_maximum_fusion.13), channel_id=1, source_target_pairs={{0,7},{1,0},{2,1},{3,2},{4,3},{5,4},{6,5},{7,6},{8,15},{9,8},{10,9... | collective-permute-start | bytes 393224 | tf_op jit(solution)/shard_map/ppermute | solution.py:408
  45.3 12.0 %collective-permute-start.6 = (f32[4,128,128]{2,1,0:T(8,128)S(1)}, f32[4,128,128]{2,1,0:T(8,128)S(1)}, u32[]{:S(2)}, u32[]{:S(2)}) collective-permute-start(f32[4,128,128]{2,1,0:T(8,128)S(1)} %pad_maximum_fusion.4), channel_id=1, source_target_pairs={{0,1},{1,2},{2,3},{3,4},{4,5},{5,6},{6,7},{7,0},{8,9},{9,10},{10,1... | collective-permute-start | bytes 786440 | tf_op jit(solution)/shard_map/ppermute | solution.py:408
  45.5 12.4 %collective-permute-start.7 = (f32[4,128,128]{2,1,0:T(8,128)S(1)}, f32[4,128,128]{2,1,0:T(8,128)S(1)}, u32[]{:S(2)}, u32[]{:S(2)}) collective-permute-start(f32[4,128,128]{2,1,0:T(8,128)S(1)} %pad_maximum_fusion.5), channel_id=1, source_target_pairs={{0,7},{1,0},{2,1},{3,2},{4,3},{5,4},{6,5},{7,6},{8,15},{9,8},{10,9... | collective-permute-start | bytes 786440 | tf_op jit(solution)/shard_map/ppermute | solution.py:408
  49.7 30.3 %collective-permute-start.10 = (f32[4,64,256]{2,1,0:T(8,128)S(1)}, f32[4,64,256]{2,1,0:T(8,128)S(1)}, u32[]{:S(2)}, u32[]{:S(2)}) collective-permute-start(f32[4,64,256]{2,1,0:T(8,128)S(1)} %get-tuple-element.46), channel_id=1, source_target_pairs={{0,8},{8,16},{16,24},{24,0},{1,9},{9,17},{17,25},{25,1},{2,10},{10... | collective-permute-start | bytes 786440 | tf_op jit(solution)/shard_map/ppermute | solution.py:408
  55.1 25.0 %collective-permute-start.11 = (f32[4,64,256]{2,1,0:T(8,128)S(1)}, f32[4,64,256]{2,1,0:T(8,128)S(1)}, u32[]{:S(2)}, u32[]{:S(2)}) collective-permute-start(f32[4,64,256]{2,1,0:T(8,128)S(1)} %get-tuple-element.47), channel_id=1, source_target_pairs={{0,24},{8,0},{16,8},{24,16},{1,25},{9,1},{17,9},{25,17},{2,26},{10... | collective-permute-start | bytes 786440 | tf_op jit(solution)/shard_map/ppermute | solution.py:408
  55.1 12.5 %collective-permute-start.13 = (f32[64,256]{1,0:T(8,128)S(1)}, f32[64,256]{1,0:T(8,128)S(1)}, u32[]{:S(2)}, u32[]{:S(2)}) collective-permute-start(f32[64,256]{1,0:T(8,128)S(1)} %get-tuple-element.67), channel_id=1, source_target_pairs={{0,8},{8,16},{16,24},{24,0},{1,9},{9,17},{17,25},{25,1},{2,10},{10... | collective-permute-start | bytes 196616 | tf_op jit(solution)/shard_map/ppermute | solution.py:487
  57.2 10.5 %collective-permute-start.14 = (f32[64,256]{1,0:T(8,128)S(1)}, f32[64,256]{1,0:T(8,128)S(1)}, u32[]{:S(2)}, u32[]{:S(2)}) collective-permute-start(f32[64,256]{1,0:T(8,128)S(1)} %get-tuple-element.69), channel_id=1, source_target_pairs={{0,16},{8,24},{16,0},{24,8},{1,17},{9,25},{17,1},{25,9},{2,18},{10... | collective-permute-start | bytes 196616 | tf_op jit(solution)/shard_map/ppermute | solution.py:487
  57.8 9.8 %collective-permute-start.15 = (f32[64,256]{1,0:T(8,128)S(1)}, f32[64,256]{1,0:T(8,128)S(1)}, u32[]{:S(2)}, u32[]{:S(2)}) collective-permute-start(f32[64,256]{1,0:T(8,128)S(1)} %get-tuple-element.68), channel_id=1, source_target_pairs={{0,24},{8,0},{16,8},{24,16},{1,25},{9,1},{17,9},{25,17},{2,26},{10... | collective-permute-start | bytes 196616 | tf_op jit(solution)/shard_map/ppermute | solution.py:487
  67.8 7.8 %collective-permute-start.17 = (f32[64,256]{1,0:T(8,128)S(1)}, f32[64,256]{1,0:T(8,128)S(1)}, u32[]{:S(2)}, u32[]{:S(2)}) collective-permute-start(f32[64,256]{1,0:T(8,128)S(1)} %fusion.11), channel_id=1, source_target_pairs={{0,4},{1,5},{2,6},{3,7},{4,0},{5,1},{6,2},{7,3},{8,12},{9,13},{10,... | collective-permute-start | bytes 196616 | tf_op jit(solution)/shard_map/ppermute | solution.py:503
  76.2 6.9 %collective-permute-start.19 = (f32[64,256]{1,0:T(8,128)S(1)}, f32[64,256]{1,0:T(8,128)S(1)}, u32[]{:S(2)}, u32[]{:S(2)}) collective-permute-start(f32[64,256]{1,0:T(8,128)S(1)} %get-tuple-element.25), channel_id=1, source_target_pairs={{0,8},{8,16},{16,24},{24,0},{1,9},{9,17},{17,25},{25,1},{2,10},{10... | collective-permute-start | bytes 196616 | tf_op jit(solution)/shard_map/ppermute | solution.py:494
  80.7 9.8 %collective-permute-start.23 = (f32[4,64,256]{2,1,0:T(8,128)S(1)}, f32[4,64,256]{2,1,0:T(8,128)S(1)}, u32[]{:S(2)}, u32[]{:S(2)}) collective-permute-start(f32[4,64,256]{2,1,0:T(8,128)S(1)} %get-tuple-element.30), channel_id=1, source_target_pairs={{0,24},{8,0},{16,8},{24,16},{1,25},{9,1},{17,9},{25,17},{2,26},{10... | collective-permute-start | bytes 786440 | tf_op jit(solution)/shard_map/ppermute | solution.py:408
  82.5 12.8 %collective-permute-start.24 = (f32[4,64,256]{2,1,0:T(8,128)S(1)}, f32[4,64,256]{2,1,0:T(8,128)S(1)}, u32[]{:S(2)}, u32[]{:S(2)}) collective-permute-start(f32[4,64,256]{2,1,0:T(8,128)S(1)} %get-tuple-element.31), channel_id=1, source_target_pairs={{0,8},{8,16},{16,24},{24,0},{1,9},{9,17},{17,25},{25,1},{2,10},{10... | collective-permute-start | bytes 786440 | tf_op jit(solution)/shard_map/ppermute | solution.py:408
  83.0 14.4 %collective-permute-start.25 = (f32[4,128,128]{2,1,0:T(8,128)S(1)}, f32[4,128,128]{2,1,0:T(8,128)S(1)}, u32[]{:S(2)}, u32[]{:S(2)}) collective-permute-start(f32[4,128,128]{2,1,0:T(8,128)S(1)} %pad_maximum_fusion.6), channel_id=1, source_target_pairs={{0,7},{1,0},{2,1},{3,2},{4,3},{5,4},{6,5},{7,6},{8,15},{9,8},{10,9... | collective-permute-start | bytes 786440 | tf_op jit(solution)/shard_map/ppermute | solution.py:408
  83.6 14.0 %collective-permute-start.26 = (f32[4,128,128]{2,1,0:T(8,128)S(1)}, f32[4,128,128]{2,1,0:T(8,128)S(1)}, u32[]{:S(2)}, u32[]{:S(2)}) collective-permute-start(f32[4,128,128]{2,1,0:T(8,128)S(1)} %pad_maximum_fusion.7), channel_id=1, source_target_pairs={{0,1},{1,2},{2,3},{3,4},{4,5},{5,6},{6,7},{7,0},{8,9},{9,10},{10,1... | collective-permute-start | bytes 786440 | tf_op jit(solution)/shard_map/ppermute | solution.py:408
  84.9 13.8 %collective-permute-start.22 = (f32[256,256]{1,0:T(8,128)S(1)}, f32[256,256]{1,0:T(8,128)S(1)}, u32[]{:S(2)}, u32[]{:S(2)}) collective-permute-start(f32[256,256]{1,0:T(8,128)S(1)} %bitcast.77), channel_id=1, source_target_pairs={{0,1},{1,0},{2,3},{3,2},{4,5},{5,4},{6,7},{7,6},{8,9},{9,8},{10,11... | collective-permute-start | bytes 786440 | tf_op jit(solution)/shard_map/ppermute | solution.py:494
  119.1 14.8 %collective-permute-start.35 = (f32[256,256]{1,0:T(8,128)S(1)}, f32[256,256]{1,0:T(8,128)S(1)}, u32[]{:S(2)}, u32[]{:S(2)}) collective-permute-start(f32[256,256]{1,0:T(8,128)S(1)} %dynamic-slice_bitcast_fusion), channel_id=1, source_target_pairs={{0,1},{1,0},{2,3},{3,2},{4,5},{5,4},{6,7},{7,6},{8,9},{9,8},{10,11... | collective-permute-start | bytes 786440 | tf_op jit(solution)/shard_map/ppermute | solution.py:487
  119.4 7.9 %collective-permute-start.31 = (f32[4,64,128]{2,1,0:T(8,128)S(1)}, f32[4,64,128]{2,1,0:T(8,128)S(1)}, u32[]{:S(2)}, u32[]{:S(2)}) collective-permute-start(f32[4,64,128]{2,1,0:T(8,128)S(1)} %pad_maximum_fusion.16), channel_id=1, source_target_pairs={{0,1},{1,2},{2,3},{3,4},{4,5},{5,6},{6,7},{7,0},{8,9},{9,10},{10,1... | collective-permute-start | bytes 393224 | tf_op jit(solution)/shard_map/ppermute | solution.py:408
  120.1 7.3 %collective-permute-start.32 = (f32[4,64,128]{2,1,0:T(8,128)S(1)}, f32[4,64,128]{2,1,0:T(8,128)S(1)}, u32[]{:S(2)}, u32[]{:S(2)}) collective-permute-start(f32[4,64,128]{2,1,0:T(8,128)S(1)} %pad_maximum_fusion.17), channel_id=1, source_target_pairs={{0,7},{1,0},{2,1},{3,2},{4,3},{5,4},{6,5},{7,6},{8,15},{9,8},{10,9... | collective-permute-start | bytes 393224 | tf_op jit(solution)/shard_map/ppermute | solution.py:408
  123.5 10.5 %collective-permute-start.29 = (f32[4,128,128]{2,1,0:T(8,128)S(1)}, f32[4,128,128]{2,1,0:T(8,128)S(1)}, u32[]{:S(2)}, u32[]{:S(2)}) collective-permute-start(f32[4,128,128]{2,1,0:T(8,128)S(1)} %pad_maximum_fusion.8), channel_id=1, source_target_pairs={{0,1},{1,2},{2,3},{3,4},{4,5},{5,6},{6,7},{7,0},{8,9},{9,10},{10,1... | collective-permute-start | bytes 786440 | tf_op jit(solution)/shard_map/ppermute | solution.py:408
  123.7 12.9 %collective-permute-start.30 = (f32[4,128,128]{2,1,0:T(8,128)S(1)}, f32[4,128,128]{2,1,0:T(8,128)S(1)}, u32[]{:S(2)}, u32[]{:S(2)}) collective-permute-start(f32[4,128,128]{2,1,0:T(8,128)S(1)} %pad_maximum_fusion.9), channel_id=1, source_target_pairs={{0,7},{1,0},{2,1},{3,2},{4,3},{5,4},{6,5},{7,6},{8,15},{9,8},{10,9... | collective-permute-start | bytes 786440 | tf_op jit(solution)/shard_map/ppermute | solution.py:408
  128.0 34.6 %collective-permute-start.33 = (f32[4,64,256]{2,1,0:T(8,128)S(1)}, f32[4,64,256]{2,1,0:T(8,128)S(1)}, u32[]{:S(2)}, u32[]{:S(2)}) collective-permute-start(f32[4,64,256]{2,1,0:T(8,128)S(1)} %get-tuple-element.38), channel_id=1, source_target_pairs={{0,8},{8,16},{16,24},{24,0},{1,9},{9,17},{17,25},{25,1},{2,10},{10... | collective-permute-start | bytes 786440 | tf_op jit(solution)/shard_map/ppermute | solution.py:408
  131.4 31.2 %collective-permute-start.34 = (f32[4,64,256]{2,1,0:T(8,128)S(1)}, f32[4,64,256]{2,1,0:T(8,128)S(1)}, u32[]{:S(2)}, u32[]{:S(2)}) collective-permute-start(f32[4,64,256]{2,1,0:T(8,128)S(1)} %get-tuple-element.39), channel_id=1, source_target_pairs={{0,24},{8,0},{16,8},{24,16},{1,25},{9,1},{17,9},{25,17},{2,26},{10... | collective-permute-start | bytes 786440 | tf_op jit(solution)/shard_map/ppermute | solution.py:408
  133.9 13.6 %collective-permute-start.36 = (f32[64,256]{1,0:T(8,128)S(1)}, f32[64,256]{1,0:T(8,128)S(1)}, u32[]{:S(2)}, u32[]{:S(2)}) collective-permute-start(f32[64,256]{1,0:T(8,128)S(1)} %get-tuple-element.54), channel_id=1, source_target_pairs={{0,8},{8,16},{16,24},{24,0},{1,9},{9,17},{17,25},{25,1},{2,10},{10... | collective-permute-start | bytes 196616 | tf_op jit(solution)/shard_map/ppermute | solution.py:487
  134.0 13.5 %collective-permute-start.37 = (f32[64,256]{1,0:T(8,128)S(1)}, f32[64,256]{1,0:T(8,128)S(1)}, u32[]{:S(2)}, u32[]{:S(2)}) collective-permute-start(f32[64,256]{1,0:T(8,128)S(1)} %get-tuple-element.56), channel_id=1, source_target_pairs={{0,16},{8,24},{16,0},{24,8},{1,17},{9,25},{17,1},{25,9},{2,18},{10... | collective-permute-start | bytes 196616 | tf_op jit(solution)/shard_map/ppermute | solution.py:487
  136.6 10.8 %collective-permute-start.38 = (f32[64,256]{1,0:T(8,128)S(1)}, f32[64,256]{1,0:T(8,128)S(1)}, u32[]{:S(2)}, u32[]{:S(2)}) collective-permute-start(f32[64,256]{1,0:T(8,128)S(1)} %get-tuple-element.55), channel_id=1, source_target_pairs={{0,24},{8,0},{16,8},{24,16},{1,25},{9,1},{17,9},{25,17},{2,26},{10... | collective-permute-start | bytes 196616 | tf_op jit(solution)/shard_map/ppermute | solution.py:487
  147.6 7.3 %collective-permute-start.40 = (f32[64,256]{1,0:T(8,128)S(1)}, f32[64,256]{1,0:T(8,128)S(1)}, u32[]{:S(2)}, u32[]{:S(2)}) collective-permute-start(f32[64,256]{1,0:T(8,128)S(1)} %fusion.9), channel_id=1, source_target_pairs={{0,4},{1,5},{2,6},{3,7},{4,0},{5,1},{6,2},{7,3},{8,12},{9,13},{10,... | collective-permute-start | bytes 196616 | tf_op jit(solution)/shard_map/ppermute | solution.py:503
  (24 other events, 123.2 us)
where the time goes:
time: 167 us; the launch traced here: 165 us
  starting transfers between devices  70.9 us (42%)
  waiting for transfers between devices  40.3 us (24%)
  Pallas kernels  28.7 us (17%)
  other arithmetic  11.3 us (7%)
  local copies, waits for them, and re-layouts  10.3 us (6%)
  between operations  3.41 us (2%)
    ppermute x24, starting transfers between devices, shifted(): lax.ppermute(value, axis, [(i, (i + step) % count) for i in range(count)])  37.9 us
    pallas_call x2, Pallas kernels, call(): pl.pallas_call(kernel, out_shape=[jax.ShapeDtypeStruct(s, f32) for s in o...  25.9 us
    ppermute x24, waiting for transfers between devices, shifted(): lax.ppermute(value, axis, [(i, (i + step) % count) for i in range(count)])  19.6 us
    ppermute x8, waiting for transfers between devices, scatter_round(): lax.ppermute(pick(s), axis, ring(axis, inner, members, s))  13.3 us
    ppermute x8, starting transfers between devices, scatter_round(): lax.ppermute(pick(s), axis, ring(axis, inner, members, s))  12.2 us
    ppermute x6, starting transfers between devices, exchange_round(): lax.ppermute(value, axis, ring(axis, inner, members, s))  11.6 us
    ppermute x8, starting transfers between devices, gather_round(): lax.ppermute(value, axis, ring(axis, inner, members, s))  9.16 us
    concatenate x16, other arithmetic, pack(): return jnp.concatenate([value[:, :rows], value[:, rows:]], axis=2)  4.63 us
  transfers between devices with their start and end apart: 46, of which 17 were waited for; matrix products, arithmetic and copies ran while one was open for 9% of the time, Pallas kernels for 2%

commit v1 on v0

--- a/solution.py
+++ b/solution.py
@@ -534,8 +534,9 @@
                 [field, plane, plane, (2, size, size)], size, 240,
             )
             peak = jnp.max(probe[0] * probe[0] + probe[1] * probe[1]) + 1e-06
-            low, high = owned_rows(grow + spread_cols(owned_cols(gcorner), size))
-            total = gcore + spread_cols(owned_cols(gcol), size) + spread_rows(low, high, size)
+            owned = owned_cols(jnp.concatenate([gcol, gcorner], axis=1))
+            low, high = owned_rows(grow + spread_cols(owned[:, size:], size))
+            total = gcore + spread_cols(owned[:, :size], size) + spread_rows(low, high, size)
             core = core - object_rate / peak * total
             summed = total_over_devices(gprobe)
             if step + 1 < ITERS:

time: 167 us -> 166 us (level); the launches traced: 165 us -> 167 us
  Pallas kernels: 28.7 us -> 15.2 us
  starting transfers between devices: 70.9 us -> 81.6 us
  other arithmetic: 11.3 us -> 14.5 us
    ppermute x8, starting transfers between devices: 12.2 us -> 33.5 us  [scatter_round(): lax.ppermute(pick(s), axis, ring(axis, inner, members, s))]
    ppermute x24 -> x20, waiting for transfers between devices: 19.6 us -> 34.1 us  [shifted(): lax.ppermute(value, axis, [(i, (i + step) % count) for i in range(count)])]
    ppermute x8, waiting for transfers between devices: 13.3 us -> 0.04 us  [scatter_round(): lax.ppermute(pick(s), axis, ring(axis, inner, members, s))]
    pallas_call x2, Pallas kernels: 25.9 us -> 13.7 us  [call(): pl.pallas_call(kernel, out_shape=[jax.ShapeDtypeStruct(s, f32) for s in o...]
    ppermute x24 -> x20, starting transfers between devices: 37.9 us -> 29.2 us  [shifted(): lax.ppermute(value, axis, [(i, (i + step) % count) for i in range(count)])]
    ppermute x6, starting transfers between devices: 11.6 us -> 7.7 us  [exchange_round(): lax.ppermute(value, axis, ring(axis, inner, members, s))]
    ppermute x8, waiting for transfers between devices: 3.68 us -> 0.02 us  [gather_round(): lax.ppermute(value, axis, ring(axis, inner, members, s))]
    ppermute x6, waiting for transfers between devices: 3.83 us -> 7.33 us  [exchange_round(): lax.ppermute(value, axis, ring(axis, inner, members, s))]
  transfers between devices with their start and end apart: 46 -> 42, of which waited for: 17 -> 17; matrix products, arithmetic and copies ran while one was open for 9% -> 12% of each run, Pallas kernels for 2% -> 1%
where the time goes in v1:
time: 166 us; the launch traced here: 167 us
  starting transfers between devices  81.6 us (49%)
  waiting for transfers between devices  41.5 us (25%)
  Pallas kernels  15.2 us (9%)
  other arithmetic  14.5 us (9%)
  local copies, waits for them, and re-layouts  10.5 us (6%)
  between operations  3.32 us (2%)
    ppermute x20, waiting for transfers between devices, shifted(): lax.ppermute(value, axis, [(i, (i + step) % count) for i in range(count)])  34.1 us
    ppermute x8, starting transfers between devices, scatter_round(): lax.ppermute(pick(s), axis, ring(axis, inner, members, s))  33.5 us
    ppermute x20, starting transfers between devices, shifted(): lax.ppermute(value, axis, [(i, (i + step) % count) for i in range(count)])  29.2 us
    pallas_call x2, Pallas kernels, call(): pl.pallas_call(kernel, out_shape=[jax.ShapeDtypeStruct(s, f32) for s in o...  13.7 us
    ppermute x8, starting transfers between devices, gather_round(): lax.ppermute(value, axis, ring(axis, inner, members, s))  11.2 us
    ppermute x6, starting transfers between devices, exchange_round(): lax.ppermute(value, axis, ring(axis, inner, members, s))  7.7 us
    ppermute x6, waiting for transfers between devices, exchange_round(): lax.ppermute(value, axis, ring(axis, inner, members, s))  7.33 us
    concatenate x12, other arithmetic, pack(): return jnp.concatenate([value[:, :rows], value[:, rows:]], axis=2)  6.06 us
  transfers between devices with their start and end apart: 42, of which 17 were waited for; matrix products, arithmetic and copies ran while one was open for 12% of the time, Pallas kernels for 1%

profile of v1, /device:TPU:0, one launch (start us, length us, event | category | flops | bytes accessed | tf_op | source)
XLA Modules:
  0.0 166.6 jit_solution(8948601408274559346)
XLA Ops:
  2.6 3.9 %collective-permute-start = (f32[4,64,256]{2,1,0:T(8,128)}, f32[4,64,256]{2,1,0:T(8,128)S(1)}, u32[]{:S(2)}, u32[]{:S(2)}) collective-permute-start(f32[4,64,256]{2,1,0:T(8,128)} %get-tuple-element.36), channel_id=1, source_target_pairs={{0,24},{8,0},{16,8},{24,16},{1,25},{9,1},{17,9},{25,17},{2,26},{10... | collective-permute-start | bytes 786440 | tf_op jit(solution)/shard_map/ppermute | solution.py:408
  7.6 2.8 %collective-permute-start.2 = (f32[4,128,128]{2,1,0:T(8,128)}, f32[4,128,128]{2,1,0:T(8,128)S(1)}, u32[]{:S(2)}, u32[]{:S(2)}) collective-permute-start(f32[4,128,128]{2,1,0:T(8,128)} %pad_maximum_fusion.6), channel_id=1, source_target_pairs={{0,7},{1,0},{2,1},{3,2},{4,3},{5,4},{6,5},{7,6},{8,15},{9,8},{10,9... | collective-permute-start | bytes 786440 | tf_op jit(solution)/shard_map/ppermute | solution.py:408
  13.6 5.4 %collective-permute-done.1 = f32[4,64,256]{2,1,0:T(8,128)} collective-permute-done((f32[4,64,256]{2,1,0:T(8,128)}, f32[4,64,256]{2,1,0:T(8,128)}, u32[]{:S(2)}, u32[]{:S(2)}) %collective-permute-start.1) | collective-permute-done | bytes 262176 | tf_op jit(solution)/shard_map/ppermute | solution.py:408
  20.2 2.2 %collective-permute-start.4 = (f32[4,64,128]{2,1,0:T(8,128)S(1)}, f32[4,64,128]{2,1,0:T(8,128)S(1)}, u32[]{:S(2)}, u32[]{:S(2)}) collective-permute-start(f32[4,64,128]{2,1,0:T(8,128)S(1)} %pad_maximum_fusion.10), channel_id=1, source_target_pairs={{0,7},{1,0},{2,1},{3,2},{4,3},{5,4},{6,5},{7,6},{8,15},{9,8},{10,9... | collective-permute-start | bytes 393224 | tf_op jit(solution)/shard_map/ppermute | solution.py:408
  25.4 3.4 %collective-permute-done.5 = f32[4,64,128]{2,1,0:T(8,128)S(1)} collective-permute-done((f32[4,64,128]{2,1,0:T(8,128)S(1)}, f32[4,64,128]{2,1,0:T(8,128)S(1)}, u32[]{:S(2)}, u32[]{:S(2)}) %collective-permute-start.5) | collective-permute-done | bytes 131104 | tf_op jit(solution)/shard_map/ppermute | solution.py:408
  29.0 6.9 %gradients.2 = (f32[4,256,256]{2,1,0:T(8,128)S(1)}, f32[4,128,256]{2,1,0:T(8,128)S(1)}, f32[4,256,128]{2,1,0:T(8,128)S(1)}, f32[4,128,128]{2,1,0:T(8,128)S(1)}, f32[2,256,256]{2,1,0:T(8,128)S(1)}) custom-call(s32[1]{0:T(128)} %bitcast.69.count_ref, s32[5,2]{1,0:T(8,128)S(1)} %copy.9.offset_ref, f32[4,256,256]{2,1,0:T(8,128)S(1)} %bitcast.73, ...), custom_call_target="tpu_custom_call" | custom-call | flops 8053063680 | bytes 8388652 | tf_op jit(solution)/shard_map/gradients/pallas_call | solution.py:392
  37.0 2.1 %collective-permute-start.10 = (f32[256,256]{1,0:T(8,128)S(1)}, f32[256,256]{1,0:T(8,128)S(1)}, u32[]{:S(2)}, u32[]{:S(2)}) collective-permute-start(f32[256,256]{1,0:T(8,128)S(1)} %dynamic-slice_bitcast_fusion.1), channel_id=1, source_target_pairs={{0,1},{1,0},{2,3},{3,2},{4,5},{5,4},{6,7},{7,6},{8,9},{9,8},{10,11... | collective-permute-start | bytes 786440 | tf_op jit(solution)/shard_map/ppermute | solution.py:487
  40.3 6.1 %collective-permute-start.11 = (f32[64,256]{1,0:T(8,128)S(1)}, f32[64,256]{1,0:T(8,128)S(1)}, u32[]{:S(2)}, u32[]{:S(2)}) collective-permute-start(f32[64,256]{1,0:T(8,128)S(1)} %get-tuple-element.65), channel_id=1, source_target_pairs={{0,8},{8,16},{16,24},{24,0},{1,9},{9,17},{17,25},{25,1},{2,10},{10... | collective-permute-start | bytes 196616 | tf_op jit(solution)/shard_map/ppermute | solution.py:487
  46.5 6.7 %collective-permute-start.12 = (f32[64,256]{1,0:T(8,128)S(1)}, f32[64,256]{1,0:T(8,128)S(1)}, u32[]{:S(2)}, u32[]{:S(2)}) collective-permute-start(f32[64,256]{1,0:T(8,128)S(1)} %get-tuple-element.67), channel_id=1, source_target_pairs={{0,16},{8,24},{16,0},{24,8},{1,17},{9,25},{17,1},{25,9},{2,18},{10... | collective-permute-start | bytes 196616 | tf_op jit(solution)/shard_map/ppermute | solution.py:487
  55.5 2.2 %collective-permute-start.7 = (f32[4,192,128]{2,1,0:T(8,128)}, f32[4,192,128]{2,1,0:T(8,128)S(1)}, u32[]{:S(2)}, u32[]{:S(2)}) collective-permute-start(f32[4,192,128]{2,1,0:T(8,128)} %pad_maximum_fusion.3), channel_id=1, source_target_pairs={{0,7},{1,0},{2,1},{3,2},{4,3},{5,4},{6,5},{7,6},{8,15},{9,8},{10,9... | collective-permute-start | bytes 1179656 | tf_op jit(solution)/shard_map/ppermute | solution.py:408
  59.1 2.5 %collective-permute-start.16 = (f32[64,256]{1,0:T(8,128)S(1)}, f32[64,256]{1,0:T(8,128)S(1)}, u32[]{:S(2)}, u32[]{:S(2)}) collective-permute-start(f32[64,256]{1,0:T(8,128)S(1)} %fusion.11), channel_id=1, source_target_pairs={{0,6},{1,7},{2,0},{3,1},{4,2},{5,3},{6,4},{7,5},{8,14},{9,15},{10,... | collective-permute-start | bytes 196616 | tf_op jit(solution)/shard_map/ppermute | solution.py:503
  62.9 2.7 %collective-permute-done.14 = f32[64,256]{1,0:T(8,128)S(1)} collective-permute-done((f32[64,256]{1,0:T(8,128)S(1)}, f32[64,256]{1,0:T(8,128)S(1)}, u32[]{:S(2)}, u32[]{:S(2)}) %collective-permute-start.14) | collective-permute-done | bytes 65568 | tf_op jit(solution)/shard_map/ppermute | solution.py:503
  67.5 3.4 %collective-permute-start.18 = (f32[64,256]{1,0:T(8,128)S(1)}, f32[64,256]{1,0:T(8,128)S(1)}, u32[]{:S(2)}, u32[]{:S(2)}) collective-permute-start(f32[64,256]{1,0:T(8,128)S(1)} %get-tuple-element.25), channel_id=1, source_target_pairs={{0,16},{8,24},{16,0},{24,8},{1,17},{9,25},{17,1},{25,9},{2,18},{10... | collective-permute-start | bytes 196616 | tf_op jit(solution)/shard_map/ppermute | solution.py:494
  73.5 2.3 %collective-permute-start.9 = (f32[4,64,256]{2,1,0:T(8,128)S(1)}, f32[4,64,256]{2,1,0:T(8,128)S(1)}, u32[]{:S(2)}, u32[]{:S(2)}) collective-permute-start(f32[4,64,256]{2,1,0:T(8,128)S(1)} %get-tuple-element.51), channel_id=1, source_target_pairs={{0,24},{8,0},{16,8},{24,16},{1,25},{9,1},{17,9},{25,17},{2,26},{10... | collective-permute-start | bytes 786440 | tf_op jit(solution)/shard_map/ppermute | solution.py:408
  76.9 4.2 %collective-permute-done.8 = f32[4,64,256]{2,1,0:T(8,128)S(1)} collective-permute-done((f32[4,64,256]{2,1,0:T(8,128)S(1)}, f32[4,64,256]{2,1,0:T(8,128)S(1)}, u32[]{:S(2)}, u32[]{:S(2)}) %collective-permute-start.8) | collective-permute-done | bytes 262176 | tf_op jit(solution)/shard_map/ppermute | solution.py:408
  81.1 2.8 %collective-permute-done.9 = f32[4,64,256]{2,1,0:T(8,128)S(1)} collective-permute-done((f32[4,64,256]{2,1,0:T(8,128)S(1)}, f32[4,64,256]{2,1,0:T(8,128)S(1)}, u32[]{:S(2)}, u32[]{:S(2)}) %collective-permute-start.9) | collective-permute-done | bytes 262176 | tf_op jit(solution)/shard_map/ppermute | solution.py:408
  86.7 3.2 %collective-permute-start.23 = (f32[4,128,128]{2,1,0:T(8,128)S(1)}, f32[4,128,128]{2,1,0:T(8,128)S(1)}, u32[]{:S(2)}, u32[]{:S(2)}) collective-permute-start(f32[4,128,128]{2,1,0:T(8,128)S(1)} %pad_maximum_fusion.8), channel_id=1, source_target_pairs={{0,7},{1,0},{2,1},{3,2},{4,3},{5,4},{6,5},{7,6},{8,15},{9,8},{10,9... | collective-permute-start | bytes 786440 | tf_op jit(solution)/shard_map/ppermute | solution.py:408
  92.0 3.1 %collective-permute-done.22 = f32[4,64,256]{2,1,0:T(8,128)S(1)} collective-permute-done((f32[4,64,256]{2,1,0:T(8,128)S(1)}, f32[4,64,256]{2,1,0:T(8,128)S(1)}, u32[]{:S(2)}, u32[]{:S(2)}) %collective-permute-start.22) | collective-permute-done | bytes 262176 | tf_op jit(solution)/shard_map/ppermute | solution.py:408
  95.3 4.4 %collective-permute-start.25 = (f32[4,64,128]{2,1,0:T(8,128)S(1)}, f32[4,64,128]{2,1,0:T(8,128)S(1)}, u32[]{:S(2)}, u32[]{:S(2)}) collective-permute-start(f32[4,64,128]{2,1,0:T(8,128)S(1)} %pad_maximum_fusion.12), channel_id=1, source_target_pairs={{0,7},{1,0},{2,1},{3,2},{4,3},{5,4},{6,5},{7,6},{8,15},{9,8},{10,9... | collective-permute-start | bytes 393224 | tf_op jit(solution)/shard_map/ppermute | solution.py:408
  100.4 3.0 %collective-permute-done.25 = f32[4,64,128]{2,1,0:T(8,128)S(1)} collective-permute-done((f32[4,64,128]{2,1,0:T(8,128)S(1)}, f32[4,64,128]{2,1,0:T(8,128)S(1)}, u32[]{:S(2)}, u32[]{:S(2)}) %collective-permute-start.25) | collective-permute-done | bytes 131104 | tf_op jit(solution)/shard_map/ppermute | solution.py:408
  103.5 3.5 %collective-permute-done.26 = f32[4,64,128]{2,1,0:T(8,128)S(1)} collective-permute-done((f32[4,64,128]{2,1,0:T(8,128)S(1)}, f32[4,64,128]{2,1,0:T(8,128)S(1)}, u32[]{:S(2)}, u32[]{:S(2)}) %collective-permute-start.26) | collective-permute-done | bytes 131104 | tf_op jit(solution)/shard_map/ppermute | solution.py:408
  107.2 6.8 %gradients.3 = (f32[4,256,256]{2,1,0:T(8,128)S(1)}, f32[4,128,256]{2,1,0:T(8,128)S(1)}, f32[4,256,128]{2,1,0:T(8,128)S(1)}, f32[4,128,128]{2,1,0:T(8,128)S(1)}, f32[2,256,256]{2,1,0:T(8,128)S(1)}) custom-call(s32[1]{0:T(128)} %bitcast.70.count_ref, s32[5,2]{1,0:T(8,128)S(1)} %copy.9.offset_ref, f32[4,256,256]{2,1,0:T(8,128)S(1)} %fusion.2.core_ref, ...), custom_call_target="tpu_custom_call" | custom-call | flops 8053063680 | bytes 8388652 | tf_op jit(solution)/shard_map/gradients/pallas_call | solution.py:392
  114.3 2.5 %collective-permute-start.31 = (f32[256,256]{1,0:T(8,128)S(1)}, f32[256,256]{1,0:T(8,128)S(1)}, u32[]{:S(2)}, u32[]{:S(2)}) collective-permute-start(f32[256,256]{1,0:T(8,128)S(1)} %dynamic-slice_bitcast_fusion), channel_id=1, source_target_pairs={{0,1},{1,0},{2,3},{3,2},{4,5},{5,4},{6,7},{7,6},{8,9},{9,8},{10,11... | collective-permute-start | bytes 786440 | tf_op jit(solution)/shard_map/ppermute | solution.py:487
  118.0 5.6 %collective-permute-start.32 = (f32[64,256]{1,0:T(8,128)S(1)}, f32[64,256]{1,0:T(8,128)S(1)}, u32[]{:S(2)}, u32[]{:S(2)}) collective-permute-start(f32[64,256]{1,0:T(8,128)S(1)} %get-tuple-element.62), channel_id=1, source_target_pairs={{0,8},{8,16},{16,24},{24,0},{1,9},{9,17},{17,25},{25,1},{2,10},{10... | collective-permute-start | bytes 196616 | tf_op jit(solution)/shard_map/ppermute | solution.py:487
  123.6 7.6 %collective-permute-start.33 = (f32[64,256]{1,0:T(8,128)S(1)}, f32[64,256]{1,0:T(8,128)S(1)}, u32[]{:S(2)}, u32[]{:S(2)}) collective-permute-start(f32[64,256]{1,0:T(8,128)S(1)} %get-tuple-element.64), channel_id=1, source_target_pairs={{0,16},{8,24},{16,0},{24,8},{1,17},{9,25},{17,1},{25,9},{2,18},{10... | collective-permute-start | bytes 196616 | tf_op jit(solution)/shard_map/ppermute | solution.py:487
  133.6 2.2 %collective-permute-start.28 = (f32[4,192,128]{2,1,0:T(8,128)}, f32[4,192,128]{2,1,0:T(8,128)}, u32[]{:S(2)}, u32[]{:S(2)}) collective-permute-start(f32[4,192,128]{2,1,0:T(8,128)} %pad_maximum_fusion.5), channel_id=1, source_target_pairs={{0,7},{1,0},{2,1},{3,2},{4,3},{5,4},{6,5},{7,6},{8,15},{9,8},{10,9... | collective-permute-start | bytes 1179656 | tf_op jit(solution)/shard_map/ppermute | solution.py:408
  138.0 2.4 %collective-permute-start.37 = (f32[64,256]{1,0:T(8,128)}, f32[64,256]{1,0:T(8,128)}, u32[]{:S(2)}, u32[]{:S(2)}) collective-permute-start(f32[64,256]{1,0:T(8,128)} %fusion.9), channel_id=1, source_target_pairs={{0,6},{1,7},{2,0},{3,1},{4,2},{5,3},{6,4},{7,5},{8,14},{9,15},{10,... | collective-permute-start | bytes 196616 | tf_op jit(solution)/shard_map/ppermute | solution.py:503
  141.7 2.0 %collective-permute-done.35 = f32[64,256]{1,0:T(8,128)} collective-permute-done((f32[64,256]{1,0:T(8,128)}, f32[64,256]{1,0:T(8,128)}, u32[]{:S(2)}, u32[]{:S(2)}) %collective-permute-start.35) | collective-permute-done | bytes 65568 | tf_op jit(solution)/shard_map/ppermute | solution.py:503
  147.2 3.0 %collective-permute-start.39 = (f32[64,256]{1,0:T(8,128)S(1)}, f32[64,256]{1,0:T(8,128)S(1)}, u32[]{:S(2)}, u32[]{:S(2)}) collective-permute-start(f32[64,256]{1,0:T(8,128)S(1)} %get-tuple-element.23), channel_id=1, source_target_pairs={{0,16},{8,24},{16,0},{24,8},{1,17},{9,25},{17,1},{25,9},{2,18},{10... | collective-permute-start | bytes 196616 | tf_op jit(solution)/shard_map/ppermute | solution.py:494
  153.6 2.4 %collective-permute-start.30 = (f32[4,64,256]{2,1,0:T(8,128)S(1)}, f32[4,64,256]{2,1,0:T(8,128)S(1)}, u32[]{:S(2)}, u32[]{:S(2)}) collective-permute-start(f32[4,64,256]{2,1,0:T(8,128)S(1)} %get-tuple-element.47), channel_id=1, source_target_pairs={{0,24},{8,0},{16,8},{24,16},{1,25},{9,1},{17,9},{25,17},{2,26},{10... | collective-permute-start | bytes 786440 | tf_op jit(solution)/shard_map/ppermute | solution.py:408
  158.2 2.9 %collective-permute-done.29 = f32[4,64,256]{2,1,0:T(8,128)S(1)} collective-permute-done((f32[4,64,256]{2,1,0:T(8,128)S(1)}, f32[4,64,256]{2,1,0:T(8,128)S(1)}, u32[]{:S(2)}, u32[]{:S(2)}) %collective-permute-start.29) | collective-permute-done | bytes 262176 | tf_op jit(solution)/shard_map/ppermute | solution.py:408
  161.0 3.3 %collective-permute-done.30 = f32[4,64,256]{2,1,0:T(8,128)S(1)} collective-permute-done((f32[4,64,256]{2,1,0:T(8,128)S(1)}, f32[4,64,256]{2,1,0:T(8,128)S(1)}, u32[]{:S(2)}, u32[]{:S(2)}) %collective-permute-start.30) | collective-permute-done | bytes 262176 | tf_op jit(solution)/shard_map/ppermute | solution.py:408
  (168 shorter events, 46.0 us)
Async XLA Ops:
  2.6 10.9 %collective-permute-start = (f32[4,64,256]{2,1,0:T(8,128)}, f32[4,64,256]{2,1,0:T(8,128)S(1)}, u32[]{:S(2)}, u32[]{:S(2)}) collective-permute-start(f32[4,64,256]{2,1,0:T(8,128)} %get-tuple-element.36), channel_id=1, source_target_pairs={{0,24},{8,0},{16,8},{24,16},{1,25},{9,1},{17,9},{25,17},{2,26},{10... | collective-permute-start | bytes 786440 | tf_op jit(solution)/shard_map/ppermute | solution.py:408
  6.5 12.5 %collective-permute-start.1 = (f32[4,64,256]{2,1,0:T(8,128)}, f32[4,64,256]{2,1,0:T(8,128)}, u32[]{:S(2)}, u32[]{:S(2)}) collective-permute-start(f32[4,64,256]{2,1,0:T(8,128)} %get-tuple-element.37), channel_id=1, source_target_pairs={{0,8},{8,16},{16,24},{24,0},{1,9},{9,17},{17,25},{25,1},{2,10},{10... | collective-permute-start | bytes 786440 | tf_op jit(solution)/shard_map/ppermute | solution.py:408
  7.6 15.0 %collective-permute-start.2 = (f32[4,128,128]{2,1,0:T(8,128)}, f32[4,128,128]{2,1,0:T(8,128)S(1)}, u32[]{:S(2)}, u32[]{:S(2)}) collective-permute-start(f32[4,128,128]{2,1,0:T(8,128)} %pad_maximum_fusion.6), channel_id=1, source_target_pairs={{0,7},{1,0},{2,1},{3,2},{4,3},{5,4},{6,5},{7,6},{8,15},{9,8},{10,9... | collective-permute-start | bytes 786440 | tf_op jit(solution)/shard_map/ppermute | solution.py:408
  11.2 11.5 %collective-permute-start.3 = (f32[4,128,128]{2,1,0:T(8,128)}, f32[4,128,128]{2,1,0:T(8,128)S(1)}, u32[]{:S(2)}, u32[]{:S(2)}) collective-permute-start(f32[4,128,128]{2,1,0:T(8,128)} %pad_maximum_fusion.7), channel_id=1, source_target_pairs={{0,1},{1,2},{2,3},{3,4},{4,5},{5,6},{6,7},{7,0},{8,9},{9,10},{10,1... | collective-permute-start | bytes 786440 | tf_op jit(solution)/shard_map/ppermute | solution.py:408
  40.2 32.1 %collective-permute-start.6 = (f32[4,192,128]{2,1,0:T(8,128)}, f32[4,192,128]{2,1,0:T(8,128)S(1)}, u32[]{:S(2)}, u32[]{:S(2)}) collective-permute-start(f32[4,192,128]{2,1,0:T(8,128)} %pad_maximum_fusion.2), channel_id=1, source_target_pairs={{0,1},{1,2},{2,3},{3,4},{4,5},{5,6},{6,7},{7,0},{8,9},{9,10},{10,1... | collective-permute-start | bytes 1179656 | tf_op jit(solution)/shard_map/ppermute | solution.py:408
  40.3 17.3 %collective-permute-start.11 = (f32[64,256]{1,0:T(8,128)S(1)}, f32[64,256]{1,0:T(8,128)S(1)}, u32[]{:S(2)}, u32[]{:S(2)}) collective-permute-start(f32[64,256]{1,0:T(8,128)S(1)} %get-tuple-element.65), channel_id=1, source_target_pairs={{0,8},{8,16},{16,24},{24,0},{1,9},{9,17},{17,25},{25,1},{2,10},{10... | collective-permute-start | bytes 196616 | tf_op jit(solution)/shard_map/ppermute | solution.py:487
  46.5 11.2 %collective-permute-start.12 = (f32[64,256]{1,0:T(8,128)S(1)}, f32[64,256]{1,0:T(8,128)S(1)}, u32[]{:S(2)}, u32[]{:S(2)}) collective-permute-start(f32[64,256]{1,0:T(8,128)S(1)} %get-tuple-element.67), channel_id=1, source_target_pairs={{0,16},{8,24},{16,0},{24,8},{1,17},{9,25},{17,1},{25,9},{2,18},{10... | collective-permute-start | bytes 196616 | tf_op jit(solution)/shard_map/ppermute | solution.py:487
  55.5 17.1 %collective-permute-start.7 = (f32[4,192,128]{2,1,0:T(8,128)}, f32[4,192,128]{2,1,0:T(8,128)S(1)}, u32[]{:S(2)}, u32[]{:S(2)}) collective-permute-start(f32[4,192,128]{2,1,0:T(8,128)} %pad_maximum_fusion.3), channel_id=1, source_target_pairs={{0,7},{1,0},{2,1},{3,2},{4,3},{5,4},{6,5},{7,6},{8,15},{9,8},{10,9... | collective-permute-start | bytes 1179656 | tf_op jit(solution)/shard_map/ppermute | solution.py:408
  57.7 7.8 %collective-permute-start.14 = (f32[64,256]{1,0:T(8,128)S(1)}, f32[64,256]{1,0:T(8,128)S(1)}, u32[]{:S(2)}, u32[]{:S(2)}) collective-permute-start(f32[64,256]{1,0:T(8,128)S(1)} %fusion.11), channel_id=1, source_target_pairs={{0,2},{1,3},{2,4},{3,5},{4,6},{5,7},{6,0},{7,1},{8,10},{9,11},{10,... | collective-permute-start | bytes 196616 | tf_op jit(solution)/shard_map/ppermute | solution.py:503
  57.8 8.3 %collective-permute-start.15 = (f32[64,256]{1,0:T(8,128)S(1)}, f32[64,256]{1,0:T(8,128)S(1)}, u32[]{:S(2)}, u32[]{:S(2)}) collective-permute-start(f32[64,256]{1,0:T(8,128)S(1)} %fusion.11), channel_id=1, source_target_pairs={{0,4},{1,5},{2,6},{3,7},{4,0},{5,1},{6,2},{7,3},{8,12},{9,13},{10,... | collective-permute-start | bytes 196616 | tf_op jit(solution)/shard_map/ppermute | solution.py:503
  59.1 7.6 %collective-permute-start.16 = (f32[64,256]{1,0:T(8,128)S(1)}, f32[64,256]{1,0:T(8,128)S(1)}, u32[]{:S(2)}, u32[]{:S(2)}) collective-permute-start(f32[64,256]{1,0:T(8,128)S(1)} %fusion.11), channel_id=1, source_target_pairs={{0,6},{1,7},{2,0},{3,1},{4,2},{5,3},{6,4},{7,5},{8,14},{9,15},{10,... | collective-permute-start | bytes 196616 | tf_op jit(solution)/shard_map/ppermute | solution.py:503
  66.8 9.8 %collective-permute-start.17 = (f32[64,256]{1,0:T(8,128)S(1)}, f32[64,256]{1,0:T(8,128)S(1)}, u32[]{:S(2)}, u32[]{:S(2)}) collective-permute-start(f32[64,256]{1,0:T(8,128)S(1)} %get-tuple-element.25), channel_id=1, source_target_pairs={{0,8},{8,16},{16,24},{24,0},{1,9},{9,17},{17,25},{25,1},{2,10},{10... | collective-permute-start | bytes 196616 | tf_op jit(solution)/shard_map/ppermute | solution.py:494
  67.5 9.2 %collective-permute-start.18 = (f32[64,256]{1,0:T(8,128)S(1)}, f32[64,256]{1,0:T(8,128)S(1)}, u32[]{:S(2)}, u32[]{:S(2)}) collective-permute-start(f32[64,256]{1,0:T(8,128)S(1)} %get-tuple-element.25), channel_id=1, source_target_pairs={{0,16},{8,24},{16,0},{24,8},{1,17},{9,25},{17,1},{25,9},{2,18},{10... | collective-permute-start | bytes 196616 | tf_op jit(solution)/shard_map/ppermute | solution.py:494
  72.8 8.2 %collective-permute-start.8 = (f32[4,64,256]{2,1,0:T(8,128)S(1)}, f32[4,64,256]{2,1,0:T(8,128)S(1)}, u32[]{:S(2)}, u32[]{:S(2)}) collective-permute-start(f32[4,64,256]{2,1,0:T(8,128)S(1)} %get-tuple-element.50), channel_id=1, source_target_pairs={{0,8},{8,16},{16,24},{24,0},{1,9},{9,17},{17,25},{25,1},{2,10},{10... | collective-permute-start | bytes 786440 | tf_op jit(solution)/shard_map/ppermute | solution.py:408
  73.5 10.4 %collective-permute-start.9 = (f32[4,64,256]{2,1,0:T(8,128)S(1)}, f32[4,64,256]{2,1,0:T(8,128)S(1)}, u32[]{:S(2)}, u32[]{:S(2)}) collective-permute-start(f32[4,64,256]{2,1,0:T(8,128)S(1)} %get-tuple-element.51), channel_id=1, source_target_pairs={{0,24},{8,0},{16,8},{24,16},{1,25},{9,1},{17,9},{25,17},{2,26},{10... | collective-permute-start | bytes 786440 | tf_op jit(solution)/shard_map/ppermute | solution.py:408
  76.8 13.4 %collective-permute-start.20 = (f32[256,256]{1,0:T(8,128)S(1)}, f32[256,256]{1,0:T(8,128)S(1)}, u32[]{:S(2)}, u32[]{:S(2)}) collective-permute-start(f32[256,256]{1,0:T(8,128)S(1)} %bitcast.77), channel_id=1, source_target_pairs={{0,1},{1,0},{2,3},{3,2},{4,5},{5,4},{6,7},{7,6},{8,9},{9,8},{10,11... | collective-permute-start | bytes 786440 | tf_op jit(solution)/shard_map/ppermute | solution.py:494
  84.5 7.4 %collective-permute-start.21 = (f32[4,64,256]{2,1,0:T(8,128)S(1)}, f32[4,64,256]{2,1,0:T(8,128)S(1)}, u32[]{:S(2)}, u32[]{:S(2)}) collective-permute-start(f32[4,64,256]{2,1,0:T(8,128)S(1)} %get-tuple-element.30), channel_id=1, source_target_pairs={{0,24},{8,0},{16,8},{24,16},{1,25},{9,1},{17,9},{25,17},{2,26},{10... | collective-permute-start | bytes 786440 | tf_op jit(solution)/shard_map/ppermute | solution.py:408
  85.4 9.7 %collective-permute-start.22 = (f32[4,64,256]{2,1,0:T(8,128)S(1)}, f32[4,64,256]{2,1,0:T(8,128)S(1)}, u32[]{:S(2)}, u32[]{:S(2)}) collective-permute-start(f32[4,64,256]{2,1,0:T(8,128)S(1)} %get-tuple-element.31), channel_id=1, source_target_pairs={{0,8},{8,16},{16,24},{24,0},{1,9},{9,17},{17,25},{25,1},{2,10},{10... | collective-permute-start | bytes 786440 | tf_op jit(solution)/shard_map/ppermute | solution.py:408
  86.7 13.2 %collective-permute-start.23 = (f32[4,128,128]{2,1,0:T(8,128)S(1)}, f32[4,128,128]{2,1,0:T(8,128)S(1)}, u32[]{:S(2)}, u32[]{:S(2)}) collective-permute-start(f32[4,128,128]{2,1,0:T(8,128)S(1)} %pad_maximum_fusion.8), channel_id=1, source_target_pairs={{0,7},{1,0},{2,1},{3,2},{4,3},{5,4},{6,5},{7,6},{8,15},{9,8},{10,9... | collective-permute-start | bytes 786440 | tf_op jit(solution)/shard_map/ppermute | solution.py:408
  90.1 9.9 %collective-permute-start.24 = (f32[4,128,128]{2,1,0:T(8,128)S(1)}, f32[4,128,128]{2,1,0:T(8,128)S(1)}, u32[]{:S(2)}, u32[]{:S(2)}) collective-permute-start(f32[4,128,128]{2,1,0:T(8,128)S(1)} %pad_maximum_fusion.9), channel_id=1, source_target_pairs={{0,1},{1,2},{2,3},{3,4},{4,5},{5,6},{6,7},{7,0},{8,9},{9,10},{10,1... | collective-permute-start | bytes 786440 | tf_op jit(solution)/shard_map/ppermute | solution.py:408
  95.3 8.1 %collective-permute-start.25 = (f32[4,64,128]{2,1,0:T(8,128)S(1)}, f32[4,64,128]{2,1,0:T(8,128)S(1)}, u32[]{:S(2)}, u32[]{:S(2)}) collective-permute-start(f32[4,64,128]{2,1,0:T(8,128)S(1)} %pad_maximum_fusion.12), channel_id=1, source_target_pairs={{0,7},{1,0},{2,1},{3,2},{4,3},{5,4},{6,5},{7,6},{8,15},{9,8},{10,9... | collective-permute-start | bytes 393224 | tf_op jit(solution)/shard_map/ppermute | solution.py:408
  117.9 33.7 %collective-permute-start.27 = (f32[4,192,128]{2,1,0:T(8,128)}, f32[4,192,128]{2,1,0:T(8,128)S(1)}, u32[]{:S(2)}, u32[]{:S(2)}) collective-permute-start(f32[4,192,128]{2,1,0:T(8,128)} %pad_maximum_fusion.4), channel_id=1, source_target_pairs={{0,1},{1,2},{2,3},{3,4},{4,5},{5,6},{6,7},{7,0},{8,9},{9,10},{10,1... | collective-permute-start | bytes 1179656 | tf_op jit(solution)/shard_map/ppermute | solution.py:408
  118.0 17.8 %collective-permute-start.32 = (f32[64,256]{1,0:T(8,128)S(1)}, f32[64,256]{1,0:T(8,128)S(1)}, u32[]{:S(2)}, u32[]{:S(2)}) collective-permute-start(f32[64,256]{1,0:T(8,128)S(1)} %get-tuple-element.62), channel_id=1, source_target_pairs={{0,8},{8,16},{16,24},{24,0},{1,9},{9,17},{17,25},{25,1},{2,10},{10... | collective-permute-start | bytes 196616 | tf_op jit(solution)/shard_map/ppermute | solution.py:487
  123.6 12.2 %collective-permute-start.33 = (f32[64,256]{1,0:T(8,128)S(1)}, f32[64,256]{1,0:T(8,128)S(1)}, u32[]{:S(2)}, u32[]{:S(2)}) collective-permute-start(f32[64,256]{1,0:T(8,128)S(1)} %get-tuple-element.64), channel_id=1, source_target_pairs={{0,16},{8,24},{16,0},{24,8},{1,17},{9,25},{17,1},{25,9},{2,18},{10... | collective-permute-start | bytes 196616 | tf_op jit(solution)/shard_map/ppermute | solution.py:487
  133.6 18.1 %collective-permute-start.28 = (f32[4,192,128]{2,1,0:T(8,128)}, f32[4,192,128]{2,1,0:T(8,128)}, u32[]{:S(2)}, u32[]{:S(2)}) collective-permute-start(f32[4,192,128]{2,1,0:T(8,128)} %pad_maximum_fusion.5), channel_id=1, source_target_pairs={{0,7},{1,0},{2,1},{3,2},{4,3},{5,4},{6,5},{7,6},{8,15},{9,8},{10,9... | collective-permute-start | bytes 1179656 | tf_op jit(solution)/shard_map/ppermute | solution.py:408
  136.5 8.5 %collective-permute-start.36 = (f32[64,256]{1,0:T(8,128)}, f32[64,256]{1,0:T(8,128)}, u32[]{:S(2)}, u32[]{:S(2)}) collective-permute-start(f32[64,256]{1,0:T(8,128)} %fusion.9), channel_id=1, source_target_pairs={{0,4},{1,5},{2,6},{3,7},{4,0},{5,1},{6,2},{7,3},{8,12},{9,13},{10,... | collective-permute-start | bytes 196616 | tf_op jit(solution)/shard_map/ppermute | solution.py:503
  146.1 11.9 %collective-permute-start.38 = (f32[64,256]{1,0:T(8,128)S(1)}, f32[64,256]{1,0:T(8,128)S(1)}, u32[]{:S(2)}, u32[]{:S(2)}) collective-permute-start(f32[64,256]{1,0:T(8,128)S(1)} %get-tuple-element.23), channel_id=1, source_target_pairs={{0,8},{8,16},{16,24},{24,0},{1,9},{9,17},{17,25},{25,1},{2,10},{10... | collective-permute-start | bytes 196616 | tf_op jit(solution)/shard_map/ppermute | solution.py:494
  147.2 10.8 %collective-permute-start.39 = (f32[64,256]{1,0:T(8,128)S(1)}, f32[64,256]{1,0:T(8,128)S(1)}, u32[]{:S(2)}, u32[]{:S(2)}) collective-permute-start(f32[64,256]{1,0:T(8,128)S(1)} %get-tuple-element.23), channel_id=1, source_target_pairs={{0,16},{8,24},{16,0},{24,8},{1,17},{9,25},{17,1},{25,9},{2,18},{10... | collective-permute-start | bytes 196616 | tf_op jit(solution)/shard_map/ppermute | solution.py:494
  150.1 7.9 %collective-permute-start.40 = (f32[64,256]{1,0:T(8,128)S(1)}, f32[64,256]{1,0:T(8,128)S(1)}, u32[]{:S(2)}, u32[]{:S(2)}) collective-permute-start(f32[64,256]{1,0:T(8,128)S(1)} %get-tuple-element.23), channel_id=1, source_target_pairs={{0,24},{8,0},{16,8},{24,16},{1,25},{9,1},{17,9},{25,17},{2,26},{10... | collective-permute-start | bytes 196616 | tf_op jit(solution)/shard_map/ppermute | solution.py:494
  153.0 8.0 %collective-permute-start.29 = (f32[4,64,256]{2,1,0:T(8,128)S(1)}, f32[4,64,256]{2,1,0:T(8,128)S(1)}, u32[]{:S(2)}, u32[]{:S(2)}) collective-permute-start(f32[4,64,256]{2,1,0:T(8,128)S(1)} %get-tuple-element.46), channel_id=1, source_target_pairs={{0,8},{8,16},{16,24},{24,0},{1,9},{9,17},{17,25},{25,1},{2,10},{10... | collective-permute-start | bytes 786440 | tf_op jit(solution)/shard_map/ppermute | solution.py:408
  153.6 10.7 %collective-permute-start.30 = (f32[4,64,256]{2,1,0:T(8,128)S(1)}, f32[4,64,256]{2,1,0:T(8,128)S(1)}, u32[]{:S(2)}, u32[]{:S(2)}) collective-permute-start(f32[4,64,256]{2,1,0:T(8,128)S(1)} %get-tuple-element.47), channel_id=1, source_target_pairs={{0,24},{8,0},{16,8},{24,16},{1,25},{9,1},{17,9},{25,17},{2,26},{10... | collective-permute-start | bytes 786440 | tf_op jit(solution)/shard_map/ppermute | solution.py:408
  158.0 7.6 %collective-permute-start.41 = (f32[256,256]{1,0:T(8,128)S(1)}, f32[256,256]{1,0:T(8,128)S(1)}, u32[]{:S(2)}, u32[]{:S(2)}) collective-permute-start(f32[256,256]{1,0:T(8,128)S(1)} %bitcast.75), channel_id=1, source_target_pairs={{0,1},{1,0},{2,3},{3,2},{4,5},{5,4},{6,7},{7,6},{8,9},{9,8},{10,11... | collective-permute-start | bytes 786440 | tf_op jit(solution)/shard_map/ppermute | solution.py:494
  (21 other events, 126.0 us)
